TPU v7x, 512 devices: a whole 4x8x8 slice. The times are simulated.
512 devices in a mesh: fluid: 32 (over y, x), solid: 16 (over z, core).
Axes of the slice: x: 4, y: 8, z: 8, core: 2. Of those that a mesh axis runs over, the one named last changes fastest.
Arguments:
- earlier_thermal_state: float32 [1024, 512, 128], P('fluid', 'solid'), may hold values from -6 to 6
- thermal_inertia: float32 [1024, 512, 128], P('fluid', 'solid'), may hold values from 0.3 to 3
- boundary_energy_current: float32 [64, 262144], P(None, ('fluid', 'solid')), may hold values from -6 to 6
- jacobian_quad_factors: float32 [64, 524288], P(None, ('fluid', 'solid')), may hold values from 0.05 to 0.4
- patch_holder_liquid: int32 [524288, 1], P(('fluid', 'solid')), may hold values from 0 to 31; in each aligned block of 1024 rows (0 to 1023, 1024 to 2047, ...) at most 128 rows name the same one
- patch_slot_number: int32 [524288], P(('fluid', 'solid')), may hold values from 0 to 511
Outputs:
- thermal_state_guess: float32 [1024, 512, 128], P('fluid', 'solid')
- equation_misfit: float32 [1024, 512, 128], P('fluid', 'solid')
Inputs may be any that keep to these rules, and one draw needn't show every extreme that they name: `patch_holder_liquid`: within the rows of one device, no owner index is named by more than 128 rows; in the rows of some device one owner index is named by exactly 128 rows.
All inputs are finite; a program needn't handle non-finite values.
Results may differ from a plain program's by a relative error of at most 0.00025.
Values sent between devices are 32-bit elements; how exact they have to be, the bound alone decides.
A program may use at most 64 MiB of HBM per device.

v0:
```python
import jax
import jax.numpy as jnp
from jax import lax
from jax.sharding import Mesh
from jax.sharding import PartitionSpec as P

ITERS = 3
FLUID_SOLID = ("fluid_0", "fluid_1", "solid_0", "solid_1")
FLUID = ("fluid_0", "fluid_1")
SOLID = ("solid_0", "solid_1")


def extended(shard, sides, width):
    edges = {}
    for axis, dim in sides:
        size, length = (lax.axis_size(axis), shard.shape[dim])
        up = [(i, (i + 1) % size) for i in range(size - 1)]
        last = lax.slice_in_dim(shard, length - width, length, axis=dim)
        initial = lax.slice_in_dim(shard, 0, width, axis=dim)
        edges[dim] = (
            lax.ppermute(last, axis, up),
            lax.ppermute(initial, axis, [(b, a) for a, b in up]),
        )
    done = []
    for _, dim in sides:
        low, high = edges[dim]
        around = [(width, width) if d in done else (0, 0) for d in range(shard.ndim)]
        shard = jnp.concatenate([jnp.pad(low, around), shard, jnp.pad(high, around)], axis=dim)
        done.append(dim)
    return shard


def by_axis(shard, axes):
    for axis in axes:
        shard = lax.psum(shard, axis)
    return shard


def matrix_action(field, thermal_inertia):
    padded = extended(field, ((FLUID, 0), (SOLID, 1)), 1)
    padded = jnp.pad(padded, ((0, 0), (0, 0), (1, 1)))
    beside = padded[2:, 1:-1, 1:-1] + padded[:-2, 1:-1, 1:-1]
    beside = beside + padded[1:-1, 2:, 1:-1] + padded[1:-1, :-2, 1:-1]
    beside = beside + padded[1:-1, 1:-1, 2:] + padded[1:-1, 1:-1, :-2]
    return (6.0 + thermal_inertia) * field - beside


def paired_sums(equation_misfit, precond, image):
    return (
        by_axis(jnp.sum(equation_misfit * precond), FLUID_SOLID),
        by_axis(jnp.sum(image * precond), FLUID_SOLID),
    )


def per_device(
    earlier_thermal_state,
    thermal_inertia,
    boundary_energy_current,
    jacobian_quad_factors,
    patch_holder_liquid,
    patch_slot_number,
):
    owners = lax.axis_size(FLUID)
    owner_index = patch_holder_liquid[:, 0]
    icells = patch_slot_number.shape[0]
    bucket = 4 * icells // owners
    one_hot = (owner_index[:, None] == jnp.arange(owners, dtype=jnp.int32)[None, :]).astype(
        jnp.int32
    )
    within = jnp.sum(jnp.cumsum(one_hot, axis=0) * one_hot, axis=1) - 1
    position = owner_index * bucket + within
    request = (
        jnp.zeros((owners * bucket,), jnp.int32)
        .at[position]
        .set(patch_slot_number)
        .reshape(owners, bucket)
    )
    rows_out = jnp.take(
        boundary_energy_current,
        lax.all_to_all(request, FLUID, split_axis=0, concat_axis=0, tiled=True),
        axis=1,
    )
    received = lax.all_to_all(rows_out, FLUID, split_axis=1, concat_axis=1, tiled=True)
    picked = jnp.take(received.reshape(received.shape[0], -1), position, axis=1)
    source = jnp.sum(jacobian_quad_factors * picked, axis=0).reshape(
        earlier_thermal_state.shape[0], earlier_thermal_state.shape[1]
    )
    forcing_entries = thermal_inertia * earlier_thermal_state
    forcing_entries = forcing_entries.at[:, :, -1].add(source)
    diagonal = 6.0 + thermal_inertia
    thermal_state_guess = earlier_thermal_state
    equation_misfit = forcing_entries - matrix_action(thermal_state_guess, thermal_inertia)
    precond = equation_misfit / diagonal
    image = matrix_action(precond, thermal_inertia)
    norm_now, product = paired_sums(equation_misfit, precond, image)
    update_multiplier = norm_now / product
    update_course = precond
    along = image
    for iteration in range(ITERS):
        thermal_state_guess = thermal_state_guess + update_multiplier * update_course
        equation_misfit = equation_misfit - update_multiplier * along
        if iteration + 1 < ITERS:
            precond = equation_misfit / diagonal
            image = matrix_action(precond, thermal_inertia)
            norm_next, product = paired_sums(equation_misfit, precond, image)
            ratio = norm_next / norm_now
            update_multiplier = norm_next / (product - ratio * norm_next / update_multiplier)
            update_course = precond + ratio * update_course
            along = image + ratio * along
            norm_now = norm_next
    return (thermal_state_guess, equation_misfit)


def solution(mesh):
    finer = Mesh(mesh.devices.reshape(8, 4, 8, 2), ("fluid_0", "fluid_1", "solid_0", "solid_1"))
    placed = (
        P(FLUID, SOLID, None),
        P(FLUID, SOLID, None),
        P(None, FLUID_SOLID),
        P(None, FLUID_SOLID),
        P(FLUID_SOLID, None),
        P(FLUID_SOLID),
    )
    return jax.shard_map(
        per_device,
        mesh=finer,
        in_specs=placed,
        out_specs=(P(FLUID, SOLID, None), P(FLUID, SOLID, None)),
        check_vma=False,
    )
```

profile of v0, /device:TPU:1, one launch (start us, length us, event | category | flops | bytes accessed | tf_op | source)
XLA Modules:
  0.0 308.8 jit_solution(1398895072172932174)
XLA Ops:
  0.6 0.7 fusion.21
  1.4 9.0 %reduce-window.6 = s32[32,8,128]{2,1,0:T(8,128)S(1)} reduce-window(s32[32,8,128]{2,1,0:T(8,128)S(1)} %fusion.21, s32[]{:T(128)} %constant.66.clone.1), window={size=1x1x128 pad=0_0x0_0x127_0}, to_apply=%region_0.0 | reduce-window | flops 4161536 | bytes 262148 | tf_op jit(solution)/shard_map/reduce-window
  10.5 0.1 copy.140
  10.8 0.7 fusion.20
  11.6 0.7 and_reduce_fusion
  12.3 5.0 %scatter_custom_fusion = s32[4096]{0:T(1024)} fusion(s32[1024]{0:T(1024)S(1)} %bitcast.65, s32[1024]{0:T(1024)} %param.13, s32[]{:T(128)} %constant.66.clone.1), kind=kCustom, calls=%fused_computation.105 | custom fusion | bytes 16896 | tf_op jit(solution)/shard_map/scatter | solution.py:75
  17.4 10.5 %all-to-all-start = ((s32[32,1,128]{2,1,0:T(1,128)}), s32[32,1,128]{2,1,0:T(1,128)S(1)}, u32[]{:S(2)}, u32[]{:S(2)}) async-start(s32[32,1,128]{2,1,0:T(1,128)} %bitcast.6), calls=%async_computation | async-start | bytes 32768 | tf_op jit(solution)/shard_map/all_to_all | solution.py:80
  27.9 0.1 copy.142
  28.0 8.4 %all-to-all-done = s32[32,1,128]{2,1,0:T(1,128)S(1)} async-done(((s32[32,1,128]{2,1,0:T(1,128)}), s32[32,1,128]{2,1,0:T(1,128)S(1)}, u32[]{:S(2)}, u32[]{:S(2)}) %all-to-all-start) | async-done | bytes 16416 | tf_op jit(solution)/shard_map/all_to_all | solution.py:80
  36.4 10.8 %gather_fusion = f32[4096,64]{1,0:T(8,128)S(1)} fusion(f32[64,512]{0,1:T(8,128)S(1)} %copy.142, s32[4096]{0:T(1024)S(1)} %fusion.23), kind=kCustom, calls=%fused_computation | custom fusion | bytes 2113536 | tf_op jit(solution)/shard_map/jit(_take)/gather | solution.py:78
  47.2 0.6 copy.143
  47.8 1.1 select_bitcast_fusion
  48.9 4.8 %all-to-all-start.1 = ((f32[64,32,128]{2,0,1:T(8,128)}), f32[64,32,128]{2,0,1:T(8,128)}, u32[]{:S(2)}, u32[]{:S(2)}) async-start(f32[64,32,128]{2,0,1:T(8,128)} %select_bitcast_fusion), calls=%async_computation.1 | async-start | bytes 2097152 | tf_op jit(solution)/shard_map/all_to_all | solution.py:83
  53.7 2.9 collective-permute-start.1
  56.7 1.3 collective-permute-start
  58.0 4.6 %collective-permute-start.2 = (f32[32,1,128]{2,0,1:T(8,128)S(1)}, f32[32,1,128]{2,0,1:T(8,128)S(1)}, u32[]{:S(2)}, u32[]{:S(2)}) collective-permute-start(f32[32,1,128]{2,0,1:T(8,128)S(1)} %bitcast.72), channel_id=1, source_target_pairs={{1,0},{2,1},{3,2},{4,3},{5,4},{6,5},{7,6},{8,7},{9,8},{10,9},{11,1... | collective-permute-start | bytes 49160 | tf_op jit(solution)/shard_map/ppermute | solution.py:22
  62.6 3.9 %collective-permute-start.3 = (f32[32,1,128]{2,0,1:T(8,128)S(1)}, f32[32,1,128]{2,0,1:T(8,128)S(1)}, u32[]{:S(2)}, u32[]{:S(2)}) collective-permute-start(f32[32,1,128]{2,0,1:T(8,128)S(1)} %bitcast.68), channel_id=1, source_target_pairs={{0,1},{1,2},{2,3},{3,4},{4,5},{5,6},{6,7},{7,8},{8,9},{9,10},{10,1... | collective-permute-start | bytes 49160 | tf_op jit(solution)/shard_map/ppermute | solution.py:21
  66.5 1.0 copy.145
  67.5 0.9 constant_dynamic-update-slice_fusion.1
  68.5 1.7 select_maximum_fusion.12
  70.2 8.8 %all-to-all-done.1 = f32[64,32,128]{2,0,1:T(8,128)} async-done(((f32[64,32,128]{2,0,1:T(8,128)}), f32[64,32,128]{2,0,1:T(8,128)}, u32[]{:S(2)}, u32[]{:S(2)}) %all-to-all-start.1) | async-done | bytes 1048608 | tf_op jit(solution)/shard_map/all_to_all | solution.py:83
  79.0 1.8 copy.144
  80.8 4.0 %gather_fusion.1 = f32[1024,64]{1,0:T(8,128)} fusion(f32[64,4096]{0,1:T(8,128)S(1)} %bitcast.49, s32[1024]{0:T(1024)S(1)} %broadcast_clamp_fusion), kind=kCustom, calls=%fused_computation.1 | custom fusion | bytes 528384 | tf_op jit(solution)/shard_map/jit(_take)/gather | solution.py:84
  84.8 1.6 fusion.18
  86.5 0.3 reshape.136
  86.8 0.2 slice_add_fusion.8
  87.0 3.0 scatter-add.4
  90.1 2.3 add_divide_fusion.2
  92.4 5.9 %collective-permute-start.6 = (f32[32,1,128]{2,0,1:T(8,128)S(1)}, f32[32,1,128]{2,0,1:T(8,128)S(1)}, u32[]{:S(2)}, u32[]{:S(2)}) collective-permute-start(f32[32,1,128]{2,0,1:T(8,128)S(1)} %bitcast.73), channel_id=1, source_target_pairs={{1,0},{2,1},{3,2},{4,3},{5,4},{6,5},{7,6},{8,7},{9,8},{10,9},{11,1... | collective-permute-start | bytes 49160 | tf_op jit(solution)/shard_map/ppermute | solution.py:22
  98.4 3.9 %collective-permute-start.7 = (f32[32,1,128]{2,0,1:T(8,128)S(1)}, f32[32,1,128]{2,0,1:T(8,128)S(1)}, u32[]{:S(2)}, u32[]{:S(2)}) collective-permute-start(f32[32,1,128]{2,0,1:T(8,128)S(1)} %bitcast.69), channel_id=1, source_target_pairs={{0,1},{1,2},{2,3},{3,4},{4,5},{5,6},{6,7},{7,8},{8,9},{9,10},{10,1... | collective-permute-start | bytes 49160 | tf_op jit(solution)/shard_map/ppermute | solution.py:21
  102.3 1.3 collective-permute-start.4
  103.6 4.0 %collective-permute-start.5 = (f32[1,32,128]{2,1,0:T(8,128)S(1)}, f32[1,32,128]{2,1,0:T(8,128)S(1)}, u32[]{:S(2)}, u32[]{:S(2)}) collective-permute-start(f32[1,32,128]{2,1,0:T(8,128)S(1)} %get-tuple-element.69), channel_id=1, source_target_pairs={{0,16},{16,32},{32,48},{48,64},{64,80},{80,96},{96,112},{112,128},... | collective-permute-start | bytes 49160 | tf_op jit(solution)/shard_map/ppermute | solution.py:21
  107.6 0.8 collective-permute-done.5
  108.4 0.6 select_maximum_fusion.8
  109.0 1.1 multiply_reduce_fusion.4
  110.1 17.5 %all-reduce.17 = (f32[]{:T(128)}, f32[]{:T(128)}) all-reduce(f32[]{:T(128)} %get-tuple-element.25, f32[]{:T(128)} %get-tuple-element.24), channel_id=1, replica_groups=mesh['fluid_0'=8,'fluid_1'=4,'solid_0'=8,'solid_1'=2] {'fluid_0'}, use_global_device_ids=true, to_apply=%region_6.7 | all-reduce | flops 2 | bytes 16 | tf_op jit(solution)/shard_map/psum | solution.py:35
  127.6 6.6 %all-reduce.20 = (f32[]{:T(128)}, f32[]{:T(128)}) all-reduce(f32[]{:T(128)} %get-tuple-element.36, f32[]{:T(128)} %get-tuple-element.37), channel_id=1, replica_groups=mesh['fluid_0'=8,'fluid_1'=4,'solid_0'=8,'solid_1'=2] {'fluid_1'}, use_global_device_ids=true, to_apply=%region_7.8 | all-reduce | flops 2 | bytes 16 | tf_op jit(solution)/shard_map/psum | solution.py:35
  134.2 17.6 %all-reduce.14 = (f32[]{:T(128)}, f32[]{:T(128)}) all-reduce(f32[]{:T(128)} %get-tuple-element.42, f32[]{:T(128)} %get-tuple-element.43), channel_id=1, replica_groups=mesh['fluid_0'=8,'fluid_1'=4,'solid_0'=8,'solid_1'=2] {'solid_0'}, use_global_device_ids=true, to_apply=%region_8.9 | all-reduce | flops 2 | bytes 16 | tf_op jit(solution)/shard_map/psum | solution.py:35
  151.8 14.4 %all-reduce.23 = (f32[]{:T(128)}, f32[]{:T(128)}) all-reduce(f32[]{:T(128)} %get-tuple-element.30, f32[]{:T(128)} %get-tuple-element.31), channel_id=1, replica_groups=mesh['fluid_0'=8,'fluid_1'=4,'solid_0'=8,'solid_1'=2] {'solid_1'}, use_global_device_ids=true, to_apply=%region_9.10 | all-reduce | flops 2 | bytes 16 | tf_op jit(solution)/shard_map/psum | solution.py:35
  167.6 1.2 add_divide_fusion.1
  168.9 2.3 collective-permute-start.10
  171.1 3.3 %collective-permute-start.11 = (f32[32,1,128]{2,0,1:T(8,128)S(1)}, f32[32,1,128]{2,0,1:T(8,128)S(1)}, u32[]{:S(2)}, u32[]{:S(2)}) collective-permute-start(f32[32,1,128]{2,0,1:T(8,128)S(1)} %bitcast.70), channel_id=1, source_target_pairs={{0,1},{1,2},{2,3},{3,4},{4,5},{5,6},{6,7},{7,8},{8,9},{9,10},{10,1... | collective-permute-start | bytes 49160 | tf_op jit(solution)/shard_map/ppermute | solution.py:21
  174.5 1.3 collective-permute-start.8
  175.8 4.3 %collective-permute-start.9 = (f32[1,32,128]{2,1,0:T(8,128)S(1)}, f32[1,32,128]{2,1,0:T(8,128)S(1)}, u32[]{:S(2)}, u32[]{:S(2)}) collective-permute-start(f32[1,32,128]{2,1,0:T(8,128)S(1)} %get-tuple-element.65), channel_id=1, source_target_pairs={{0,16},{16,32},{32,48},{48,64},{64,80},{80,96},{96,112},{112,128},... | collective-permute-start | bytes 49160 | tf_op jit(solution)/shard_map/ppermute | solution.py:21
  180.1 0.8 collective-permute-done.9
  180.9 0.6 select_maximum_fusion.4
  181.5 1.9 multiply_reduce_fusion.2
  183.4 17.8 %all-reduce.16 = (f32[]{:T(128)}, f32[]{:T(128)}) all-reduce(f32[]{:T(128)} %get-tuple-element.23, f32[]{:T(128)} %get-tuple-element.22), channel_id=1, replica_groups=mesh['fluid_0'=8,'fluid_1'=4,'solid_0'=8,'solid_1'=2] {'fluid_0'}, use_global_device_ids=true, to_apply=%region_16.17 | all-reduce | flops 2 | bytes 16 | tf_op jit(solution)/shard_map/psum | solution.py:35
  201.2 6.6 %all-reduce.19 = (f32[]{:T(128)}, f32[]{:T(128)}) all-reduce(f32[]{:T(128)} %get-tuple-element.34, f32[]{:T(128)} %get-tuple-element.35), channel_id=1, replica_groups=mesh['fluid_0'=8,'fluid_1'=4,'solid_0'=8,'solid_1'=2] {'fluid_1'}, use_global_device_ids=true, to_apply=%region_17.18 | all-reduce | flops 2 | bytes 16 | tf_op jit(solution)/shard_map/psum | solution.py:35
  207.9 11.4 %all-reduce.13 = (f32[]{:T(128)}, f32[]{:T(128)}) all-reduce(f32[]{:T(128)} %get-tuple-element.40, f32[]{:T(128)} %get-tuple-element.41), channel_id=1, replica_groups=mesh['fluid_0'=8,'fluid_1'=4,'solid_0'=8,'solid_1'=2] {'solid_0'}, use_global_device_ids=true, to_apply=%region_18.19 | all-reduce | flops 2 | bytes 16 | tf_op jit(solution)/shard_map/psum | solution.py:35
  219.2 13.0 %all-reduce.22 = (f32[]{:T(128)}, f32[]{:T(128)}) all-reduce(f32[]{:T(128)} %get-tuple-element.28, f32[]{:T(128)} %get-tuple-element.29), channel_id=1, replica_groups=mesh['fluid_0'=8,'fluid_1'=4,'solid_0'=8,'solid_1'=2] {'solid_1'}, use_global_device_ids=true, to_apply=%region_19.20 | all-reduce | flops 2 | bytes 16 | tf_op jit(solution)/shard_map/psum | solution.py:35
  237.0 1.4 add_divide_fusion
  238.5 2.3 collective-permute-start.14
  240.7 3.3 %collective-permute-start.15 = (f32[32,1,128]{2,0,1:T(8,128)S(1)}, f32[32,1,128]{2,0,1:T(8,128)S(1)}, u32[]{:S(2)}, u32[]{:S(2)}) collective-permute-start(f32[32,1,128]{2,0,1:T(8,128)S(1)} %bitcast.71), channel_id=1, source_target_pairs={{0,1},{1,2},{2,3},{3,4},{4,5},{5,6},{6,7},{7,8},{8,9},{9,10},{10,1... | collective-permute-start | bytes 49160 | tf_op jit(solution)/shard_map/ppermute | solution.py:21
  244.0 1.3 collective-permute-start.12
  245.3 4.0 %collective-permute-start.13 = (f32[1,32,128]{2,1,0:T(8,128)S(1)}, f32[1,32,128]{2,1,0:T(8,128)S(1)}, u32[]{:S(2)}, u32[]{:S(2)}) collective-permute-start(f32[1,32,128]{2,1,0:T(8,128)S(1)} %get-tuple-element.61), channel_id=1, source_target_pairs={{0,16},{16,32},{32,48},{48,64},{64,80},{80,96},{96,112},{112,128},... | collective-permute-start | bytes 49160 | tf_op jit(solution)/shard_map/ppermute | solution.py:21
  249.4 0.8 collective-permute-done.13
  250.2 0.6 select_maximum_fusion
  250.8 1.9 multiply_reduce_fusion
  252.7 18.4 %all-reduce.15 = (f32[]{:T(128)}, f32[]{:T(128)}) all-reduce(f32[]{:T(128)} %get-tuple-element.21, f32[]{:T(128)} %get-tuple-element.20), channel_id=1, replica_groups=mesh['fluid_0'=8,'fluid_1'=4,'solid_0'=8,'solid_1'=2] {'fluid_0'}, use_global_device_ids=true, to_apply=%region_26.27 | all-reduce | flops 2 | bytes 16 | tf_op jit(solution)/shard_map/psum | solution.py:35
  271.1 6.6 %all-reduce.18 = (f32[]{:T(128)}, f32[]{:T(128)}) all-reduce(f32[]{:T(128)} %get-tuple-element.32, f32[]{:T(128)} %get-tuple-element.33), channel_id=1, replica_groups=mesh['fluid_0'=8,'fluid_1'=4,'solid_0'=8,'solid_1'=2] {'fluid_1'}, use_global_device_ids=true, to_apply=%region_27.28 | all-reduce | flops 2 | bytes 16 | tf_op jit(solution)/shard_map/psum | solution.py:35
  277.8 11.5 %all-reduce.12 = (f32[]{:T(128)}, f32[]{:T(128)}) all-reduce(f32[]{:T(128)} %get-tuple-element.38, f32[]{:T(128)} %get-tuple-element.39), channel_id=1, replica_groups=mesh['fluid_0'=8,'fluid_1'=4,'solid_0'=8,'solid_1'=2] {'solid_0'}, use_global_device_ids=true, to_apply=%region_28.29 | all-reduce | flops 2 | bytes 16 | tf_op jit(solution)/shard_map/psum | solution.py:35
  289.3 12.8 %all-reduce.21 = (f32[]{:T(128)}, f32[]{:T(128)}) all-reduce(f32[]{:T(128)} %get-tuple-element.26, f32[]{:T(128)} %get-tuple-element.27), channel_id=1, replica_groups=mesh['fluid_0'=8,'fluid_1'=4,'solid_0'=8,'solid_1'=2] {'solid_1'}, use_global_device_ids=true, to_apply=%region_29.30 | all-reduce | flops 2 | bytes 16 | tf_op jit(solution)/shard_map/psum | solution.py:35
  306.0 2.8 multiply_subtract_fusion
  (58 shorter events, 0.6 us)
Async XLA Ops:
  0.6 27.2 %copy-start.8 = (f32[64,512]{1,0:T(8,128)S(1)}, f32[64,512]{1,0:T(8,128)}, u32[]{:S(2)}) copy-start(f32[64,512]{1,0:T(8,128)} %param.10) | copy-start | bytes 393220
  17.4 19.0 %all-to-all-start = ((s32[32,1,128]{2,1,0:T(1,128)}), s32[32,1,128]{2,1,0:T(1,128)S(1)}, u32[]{:S(2)}, u32[]{:S(2)}) async-start(s32[32,1,128]{2,1,0:T(1,128)} %bitcast.6), calls=%async_computation | async-start | bytes 32768 | tf_op jit(solution)/shard_map/all_to_all | solution.py:80
  48.9 4.8 %copy-start.1 = (f32[32,32,128]{2,1,0:T(8,128)S(1)}, f32[32,32,128]{2,1,0:T(8,128)}, u32[]{:S(2)}) copy-start(f32[32,32,128]{2,1,0:T(8,128)} %param.8) | copy-start | bytes 1572868
  48.9 17.6 %copy-start.7 = (f32[64,1024]{1,0:T(8,128)S(1)}, f32[64,1024]{1,0:T(8,128)}, u32[]{:S(2)}) copy-start(f32[64,1024]{1,0:T(8,128)} %param.11) | copy-start | bytes 786436
  48.9 18.6 %copy-start = (f32[32,32,128]{2,1,0:T(8,128)S(1)}, f32[32,32,128]{2,1,0:T(8,128)}, u32[]{:S(2)}) copy-start(f32[32,32,128]{2,1,0:T(8,128)} %param.9) | copy-start | bytes 1572868
  48.9 30.1 %all-to-all-start.1 = ((f32[64,32,128]{2,0,1:T(8,128)}), f32[64,32,128]{2,0,1:T(8,128)}, u32[]{:S(2)}, u32[]{:S(2)}) async-start(f32[64,32,128]{2,0,1:T(8,128)} %select_bitcast_fusion), calls=%async_computation.1 | async-start | bytes 2097152 | tf_op jit(solution)/shard_map/all_to_all | solution.py:83
  53.7 13.8 %collective-permute-start.1 = (f32[1,32,128]{2,1,0:T(8,128)S(1)}, f32[1,32,128]{2,1,0:T(8,128)S(1)}, u32[]{:S(2)}, u32[]{:S(2)}) collective-permute-start(f32[1,32,128]{2,1,0:T(8,128)S(1)} %get-tuple-element.76), channel_id=1, source_target_pairs={{0,16},{16,32},{32,48},{48,64},{64,80},{80,96},{96,112},{112,128},... | collective-permute-start | bytes 49160 | tf_op jit(solution)/shard_map/ppermute | solution.py:21
  56.7 11.8 %collective-permute-start = (f32[1,32,128]{2,1,0:T(8,128)S(1)}, f32[1,32,128]{2,1,0:T(8,128)S(1)}, u32[]{:S(2)}, u32[]{:S(2)}) collective-permute-start(f32[1,32,128]{2,1,0:T(8,128)S(1)} %get-tuple-element.75), channel_id=1, source_target_pairs={{16,0},{32,16},{48,32},{64,48},{80,64},{96,80},{112,96},{128,112},... | collective-permute-start | bytes 49160 | tf_op jit(solution)/shard_map/ppermute | solution.py:22
  58.0 10.4 %collective-permute-start.2 = (f32[32,1,128]{2,0,1:T(8,128)S(1)}, f32[32,1,128]{2,0,1:T(8,128)S(1)}, u32[]{:S(2)}, u32[]{:S(2)}) collective-permute-start(f32[32,1,128]{2,0,1:T(8,128)S(1)} %bitcast.72), channel_id=1, source_target_pairs={{1,0},{2,1},{3,2},{4,3},{5,4},{6,5},{7,6},{8,7},{9,8},{10,9},{11,1... | collective-permute-start | bytes 49160 | tf_op jit(solution)/shard_map/ppermute | solution.py:22
  62.6 5.8 %collective-permute-start.3 = (f32[32,1,128]{2,0,1:T(8,128)S(1)}, f32[32,1,128]{2,0,1:T(8,128)S(1)}, u32[]{:S(2)}, u32[]{:S(2)}) collective-permute-start(f32[32,1,128]{2,0,1:T(8,128)S(1)} %bitcast.68), channel_id=1, source_target_pairs={{0,1},{1,2},{2,3},{3,4},{4,5},{5,6},{6,7},{7,8},{8,9},{9,10},{10,1... | collective-permute-start | bytes 49160 | tf_op jit(solution)/shard_map/ppermute | solution.py:21
  68.5 1.7 copy-start.6
  84.8 2.0 copy-start.5
  92.4 75.2 %copy-start.4 = (f32[32,32,128]{2,1,0:T(8,128)}, f32[32,32,128]{2,1,0:T(8,128)S(1)}, u32[]{:S(2)}) copy-start(f32[32,32,128]{2,1,0:T(8,128)S(1)} %get-tuple-element.58) | copy-start | bytes 1572868
  92.4 15.1 %collective-permute-start.6 = (f32[32,1,128]{2,0,1:T(8,128)S(1)}, f32[32,1,128]{2,0,1:T(8,128)S(1)}, u32[]{:S(2)}, u32[]{:S(2)}) collective-permute-start(f32[32,1,128]{2,0,1:T(8,128)S(1)} %bitcast.73), channel_id=1, source_target_pairs={{1,0},{2,1},{3,2},{4,3},{5,4},{6,5},{7,6},{8,7},{9,8},{10,9},{11,1... | collective-permute-start | bytes 49160 | tf_op jit(solution)/shard_map/ppermute | solution.py:22
  98.4 9.2 %collective-permute-start.7 = (f32[32,1,128]{2,0,1:T(8,128)S(1)}, f32[32,1,128]{2,0,1:T(8,128)S(1)}, u32[]{:S(2)}, u32[]{:S(2)}) collective-permute-start(f32[32,1,128]{2,0,1:T(8,128)S(1)} %bitcast.69), channel_id=1, source_target_pairs={{0,1},{1,2},{2,3},{3,4},{4,5},{5,6},{6,7},{7,8},{8,9},{9,10},{10,1... | collective-permute-start | bytes 49160 | tf_op jit(solution)/shard_map/ppermute | solution.py:21
  102.3 5.4 %collective-permute-start.4 = (f32[1,32,128]{2,1,0:T(8,128)S(1)}, f32[1,32,128]{2,1,0:T(8,128)S(1)}, u32[]{:S(2)}, u32[]{:S(2)}) collective-permute-start(f32[1,32,128]{2,1,0:T(8,128)S(1)} %get-tuple-element.70), channel_id=1, source_target_pairs={{16,0},{32,16},{48,32},{64,48},{80,64},{96,80},{112,96},{128,112},... | collective-permute-start | bytes 49160 | tf_op jit(solution)/shard_map/ppermute | solution.py:22
  103.6 4.8 %collective-permute-start.5 = (f32[1,32,128]{2,1,0:T(8,128)S(1)}, f32[1,32,128]{2,1,0:T(8,128)S(1)}, u32[]{:S(2)}, u32[]{:S(2)}) collective-permute-start(f32[1,32,128]{2,1,0:T(8,128)S(1)} %get-tuple-element.69), channel_id=1, source_target_pairs={{0,16},{16,32},{32,48},{48,64},{64,80},{80,96},{96,112},{112,128},... | collective-permute-start | bytes 49160 | tf_op jit(solution)/shard_map/ppermute | solution.py:21
  168.8 68.2 %copy-start.3 = (f32[32,32,128]{2,1,0:T(8,128)}, f32[32,32,128]{2,1,0:T(8,128)S(1)}, u32[]{:S(2)}) copy-start(f32[32,32,128]{2,1,0:T(8,128)S(1)} %get-tuple-element.55) | copy-start | bytes 1572868
  168.9 11.2 %collective-permute-start.10 = (f32[32,1,128]{2,0,1:T(8,128)S(1)}, f32[32,1,128]{2,0,1:T(8,128)S(1)}, u32[]{:S(2)}, u32[]{:S(2)}) collective-permute-start(f32[32,1,128]{2,0,1:T(8,128)S(1)} %bitcast.74), channel_id=1, source_target_pairs={{1,0},{2,1},{3,2},{4,3},{5,4},{6,5},{7,6},{8,7},{9,8},{10,9},{11,1... | collective-permute-start | bytes 49160 | tf_op jit(solution)/shard_map/ppermute | solution.py:22
  171.1 8.9 %collective-permute-start.11 = (f32[32,1,128]{2,0,1:T(8,128)S(1)}, f32[32,1,128]{2,0,1:T(8,128)S(1)}, u32[]{:S(2)}, u32[]{:S(2)}) collective-permute-start(f32[32,1,128]{2,0,1:T(8,128)S(1)} %bitcast.70), channel_id=1, source_target_pairs={{0,1},{1,2},{2,3},{3,4},{4,5},{5,6},{6,7},{7,8},{8,9},{9,10},{10,1... | collective-permute-start | bytes 49160 | tf_op jit(solution)/shard_map/ppermute | solution.py:21
  174.5 5.6 %collective-permute-start.8 = (f32[1,32,128]{2,1,0:T(8,128)S(1)}, f32[1,32,128]{2,1,0:T(8,128)S(1)}, u32[]{:S(2)}, u32[]{:S(2)}) collective-permute-start(f32[1,32,128]{2,1,0:T(8,128)S(1)} %get-tuple-element.66), channel_id=1, source_target_pairs={{16,0},{32,16},{48,32},{64,48},{80,64},{96,80},{112,96},{128,112},... | collective-permute-start | bytes 49160 | tf_op jit(solution)/shard_map/ppermute | solution.py:22
  175.8 5.1 %collective-permute-start.9 = (f32[1,32,128]{2,1,0:T(8,128)S(1)}, f32[1,32,128]{2,1,0:T(8,128)S(1)}, u32[]{:S(2)}, u32[]{:S(2)}) collective-permute-start(f32[1,32,128]{2,1,0:T(8,128)S(1)} %get-tuple-element.65), channel_id=1, source_target_pairs={{0,16},{16,32},{32,48},{48,64},{64,80},{80,96},{96,112},{112,128},... | collective-permute-start | bytes 49160 | tf_op jit(solution)/shard_map/ppermute | solution.py:21
  238.4 14.3 %copy-start.2 = (f32[32,32,128]{2,1,0:T(8,128)}, f32[32,32,128]{2,1,0:T(8,128)S(1)}, u32[]{:S(2)}) copy-start(f32[32,32,128]{2,1,0:T(8,128)S(1)} %get-tuple-element.52) | copy-start | bytes 1572868
  238.5 10.9 %collective-permute-start.14 = (f32[32,1,128]{2,0,1:T(8,128)S(1)}, f32[32,1,128]{2,0,1:T(8,128)S(1)}, u32[]{:S(2)}, u32[]{:S(2)}) collective-permute-start(f32[32,1,128]{2,0,1:T(8,128)S(1)} %bitcast.75), channel_id=1, source_target_pairs={{1,0},{2,1},{3,2},{4,3},{5,4},{6,5},{7,6},{8,7},{9,8},{10,9},{11,1... | collective-permute-start | bytes 49160 | tf_op jit(solution)/shard_map/ppermute | solution.py:22
  240.7 8.6 %collective-permute-start.15 = (f32[32,1,128]{2,0,1:T(8,128)S(1)}, f32[32,1,128]{2,0,1:T(8,128)S(1)}, u32[]{:S(2)}, u32[]{:S(2)}) collective-permute-start(f32[32,1,128]{2,0,1:T(8,128)S(1)} %bitcast.71), channel_id=1, source_target_pairs={{0,1},{1,2},{2,3},{3,4},{4,5},{5,6},{6,7},{7,8},{8,9},{9,10},{10,1... | collective-permute-start | bytes 49160 | tf_op jit(solution)/shard_map/ppermute | solution.py:21
  244.0 5.4 %collective-permute-start.12 = (f32[1,32,128]{2,1,0:T(8,128)S(1)}, f32[1,32,128]{2,1,0:T(8,128)S(1)}, u32[]{:S(2)}, u32[]{:S(2)}) collective-permute-start(f32[1,32,128]{2,1,0:T(8,128)S(1)} %get-tuple-element.62), channel_id=1, source_target_pairs={{16,0},{32,16},{48,32},{64,48},{80,64},{96,80},{112,96},{128,112},... | collective-permute-start | bytes 49160 | tf_op jit(solution)/shard_map/ppermute | solution.py:22
  245.3 4.8 %collective-permute-start.13 = (f32[1,32,128]{2,1,0:T(8,128)S(1)}, f32[1,32,128]{2,1,0:T(8,128)S(1)}, u32[]{:S(2)}, u32[]{:S(2)}) collective-permute-start(f32[1,32,128]{2,1,0:T(8,128)S(1)} %get-tuple-element.61), channel_id=1, source_target_pairs={{0,16},{16,32},{32,48},{48,64},{64,80},{80,96},{96,112},{112,128},... | collective-permute-start | bytes 49160 | tf_op jit(solution)/shard_map/ppermute | solution.py:21
where the time goes:
time: 310 us; the launch traced here: 309 us
  blocking collectives  154 us (50%)
  starting transfers between devices  65 us (21%)
  other arithmetic  31.3 us (10%)
  local copies, waits for them, and re-layouts  27.3 us (9%)
  waiting for transfers between devices  19.6 us (6%)
  between operations  11.1 us (4%)
    psum x12, blocking collectives, by_axis(): shard = lax.psum(shard, axis)  154 us
    ppermute x8, starting transfers between devices, extended(): lax.ppermute(last, axis, up)  29.6 us
    ppermute x8, starting transfers between devices, extended(): lax.ppermute(initial, axis, [(b, a) for a, b in up])  20.1 us
    gather x2, local copies, waits for them, and re-layouts, per_device(): jnp.take(boundary_energy_current, lax.all_to_all(request, FLUID, split_ax...  11.3 us
    all_to_all x1, starting transfers between devices, per_device(): lax.all_to_all(request, FLUID, split_axis=0, concat_axis=0, tiled=True)  10.5 us
    another operation x3, other arithmetic  9.15 us
    all_to_all x1, waiting for transfers between devices, per_device(): lax.all_to_all(rows_out, FLUID, split_axis=1, concat_axis=1, tiled=True)  8.82 us
    all_to_all x1, waiting for transfers between devices, per_device(): lax.all_to_all(request, FLUID, split_axis=0, concat_axis=0, tiled=True)  8.4 us
  transfers between devices with their start and end apart: 18, of which 5 were waited for; matrix products, arithmetic and copies ran while one was open for 1% of the time, Pallas kernels for 0%

commit v1 on v0

v1 whole, which is shorter than its diff:
```python
import functools

import jax
import jax.numpy as jnp
from jax import lax
from jax.experimental import pallas as pl
from jax.experimental.pallas import tpu as pltpu
from jax.sharding import PartitionSpec as P

ITERS = 3
XCHIPS = 4
CORES = 2
MESH = pl.DeviceIdType.MESH
F32 = jnp.float32
BF16 = jnp.bfloat16
AROUND = [(a, b) for a in (-1, 0, 1) for b in (-1, 0, 1) if (a, b) != (0, 0)]
LOW = 5
SIDE = 8


def iota(shape, axis):
    return lax.broadcasted_iota(jnp.int32, shape, axis)


def body(
    nx, ny, nz,
    x0_hbm, c_hbm, b_hbm, j_hbm, owner_hbm, slot_hbm,
    guess_hbm, misfit_hbm,
    xe, de, w0, w1, w2, last,
    bv, jv, idx, tabs, held, jac, codes, code_own, key, jm, acc,
    part_out, part_in, source, around_in, sum_out, sum_x, sum_y, sum_z,
    load_sem, store_sem, bx_send, bx_recv, jx_send, jx_recv, cx_send, cx_recv,
    ring_send, ring_recv, halo_send, halo_recv, px_send, px_recv,
    sh_send, sh_recv, ar_send, ar_recv,
):
    cx, cy, cz = (xe.shape[0] - 10, xe.shape[1] - 16, xe.shape[2])
    quads, faces = bv.shape
    rows = jv.shape[1]
    share = quads // nx
    many = 128 // share
    deep = faces // many
    rowsets = rows // 128
    f, s = lax.axis_index("fluid"), lax.axis_index("solid")
    nf, ns = nx * ny, nz * CORES
    x, y = lax.rem(f, nx), f // nx
    core, z = lax.rem(s, CORES), s // CORES

    def remote(src, dst, send, recv, at):
        return pltpu.make_async_remote_copy(
            src_ref=src, dst_ref=dst, send_sem=send, recv_sem=recv,
            device_id=at, device_id_type=MESH,
        )

    def beside(a, b):
        return (lax.rem(f + a + nf, nf), lax.rem(s + b + ns, ns))

    def on_x(d, flip):
        return (y * nx + lax.rem(x + d, nx), z * CORES + lax.rem(core + flip, CORES))

    def on_y(d):
        return (lax.rem(y + d, ny) * nx + x, s)

    def on_z(d):
        return (f, lax.rem(z + d, nz) * CORES + core)

    plane = [(d, flip) for d in range(nx) for flip in range(CORES) if (d, flip) != (0, 0)]

    inner = (pl.ds(LOW, cx), pl.ds(SIDE, cy))
    loads = [
        pltpu.make_async_copy(b_hbm, bv, load_sem.at[0]),
        pltpu.make_async_copy(owner_hbm, idx.at[0], load_sem.at[1]),
        pltpu.make_async_copy(slot_hbm, idx.at[1], load_sem.at[2]),
        pltpu.make_async_copy(j_hbm, jv, load_sem.at[3]),
        pltpu.make_async_copy(x0_hbm, xe.at[inner], load_sem.at[4]),
        pltpu.make_async_copy(c_hbm, de.at[inner], load_sem.at[5]),
    ]
    for load in loads:
        load.start()

    barrier = pltpu.get_barrier_semaphore()
    partners = [on_x(d, flip) for d, flip in plane]
    partners += [on_y(d) for d in range(1, ny)] + [on_z(d) for d in range(1, nz)]
    partners += [beside(a, b) for a, b in AROUND]
    for at in partners:
        pl.semaphore_signal(barrier, inc=1, device_id=at, device_id_type=MESH)

    guard = jnp.zeros(xe.shape[1:], F32)
    for ref in (xe, w0, w1, w2):
        ref[0] = guard
        ref[cx + 9] = guard

    loads[0].wait()
    for a in range(nx):
        mine = bv[a * share : (a + 1) * share, :]
        stack = jnp.concatenate(
            [mine[:, (m * deep // 128) * 128 : (m * deep // 128) * 128 + 128] for m in range(many)], axis=0
        )
        if deep < 128:
            turned = pltpu.roll(stack, 128 - deep, 1)
            odd = (iota(stack.shape, 0) // share) % 2 == 1
            stack = jnp.where(odd, turned, stack)
        tabs[a] = stack.T[:deep]
    loads[1].wait()
    loads[2].wait()
    code_own[...] = idx[0] * faces + idx[1]
    codes[0] = code_own[...]
    held[y, 0] = tabs[x]
    loads[3].wait()
    jac[0] = jv[pl.ds(pl.multiple_of(x * share, share), share), :]
    acc[...] = jnp.zeros_like(acc)
    loads[4].wait()
    loads[5].wait()

    pl.semaphore_wait(barrier, len(partners))

    spread = []
    for d in range(1, nx):
        at = on_x(d, 0)
        to = lax.rem(x + d, nx)
        spread.append(remote(tabs.at[to], held.at[y, d], bx_send.at[d - 1], bx_recv.at[d - 1], at))
        spread[-1].start()

    def ring(t, d, way):
        slot = lax.rem(y + ny + (1 - t if way == 0 else t - 1), ny)
        at = on_y(1 if way == 0 else ny - 1)
        block = held.at[slot, d]
        return remote(block, block, ring_send.at[way, t - 1, d], ring_recv.at[way, t - 1, d], at)

    half = ny // 2

    def goes(t, d, way):
        return t < half or (d < nx // 2) == (way == 0)

    ways = [
        [[ring(t, d, way) if goes(t, d, way) else None for way in range(2)] for d in range(nx)]
        for t in range(1, half + 1)
    ]

    def forward(t, d):
        if t == 1:
            if d > 0:
                spread[d - 1].wait_recv()
        else:
            for way in range(2):
                ways[t - 2][d][way].wait_recv()
        for way in range(2):
            if goes(t, d, way):
                ways[t - 1][d][way].start()

    forward(1, 0)
    coded, jacs, halos = [], [], []
    for d in range(1, nx):
        at, to = on_x(d, 0), lax.rem(x + d, nx)
        coded.append(remote(code_own, codes.at[d], cx_send.at[d - 1], cx_recv.at[d - 1], at))
        coded[-1].start()
        jacs.append(
            remote(
                jv.at[pl.ds(pl.multiple_of(to * share, share), share)], jac.at[d],
                jx_send.at[d - 1], jx_recv.at[d - 1], at,
            )
        )
        jacs[-1].start()
    to_x = {-1: (pl.ds(LOW, 4), pl.ds(LOW + cx, 4)), 0: (pl.ds(LOW, cx),) * 2, 1: (pl.ds(LOW + cx - 4, 4), pl.ds(LOW - 4, 4))}
    to_y = {-1: (pl.ds(SIDE, 8), pl.ds(SIDE + cy, 8)), 0: (pl.ds(SIDE, cy),) * 2, 1: (pl.ds(SIDE + cy - 8, 8), pl.ds(SIDE - 8, 8))}
    for n, (a, b) in enumerate(AROUND):
        for k, ref in enumerate((xe, de)):
            halos.append(
                remote(
                    ref.at[to_x[a][0], to_y[b][0]], ref.at[to_x[a][1], to_y[b][1]],
                    halo_send.at[k, n], halo_recv.at[k, n], beside(a, b),
                )
            )
            halos[-1].start()
    for d in range(1, nx):
        forward(1, d)

    def prepare(d):
        if d > 0:
            coded[d - 1].wait_recv()
            jacs[d - 1].wait_recv()

        def one(i, carry):
            code = codes[d, pl.ds(i, 1), :]
            place = pl.ds(pl.multiple_of(d * rows + i * 128, 128), 128)
            owner, slot = code // faces, lax.rem(code, faces)
            keys = (owner * deep + lax.rem(slot, deep)).astype(F32)
            key[place, :] = jnp.broadcast_to(keys, (128, 128)).T
            j = jac[d, :, pl.ds(pl.multiple_of(i * 128, 128), 128)]
            tiled = jnp.concatenate([j] * many, axis=0)
            wanted = iota((128, 128), 0) // share == jnp.broadcast_to(slot // deep, (128, 128))
            jm[place, :] = jnp.where(wanted, tiled, 0.0).T
            return carry

        lax.fori_loop(0, rowsets, one, 0)

    lane_f = iota((256, 128), 1).astype(F32)

    def weight(slot):
        parts = []
        for d in range(nx):
            parts.append(held[slot, d])
        table = jnp.concatenate(parts, axis=0)
        high = table.astype(BF16)
        low = (table - high.astype(F32)).astype(BF16)
        return jnp.concatenate([high, low], axis=1)

    def base_of(slot, d):
        return (slot * nx + lax.rem(x - d + nx, nx)) * deep

    def pick(d, slots):
        tables = [weight(slot) for slot in slots]
        lanes = iota((1, 128), 1)
        marks = []
        for slot in slots:
            for tile in range(nx * deep // 128):
                mark = jnp.zeros((1, 128), jnp.int32)
                for e in range(128 // deep):
                    p = tile * (128 // deep) + e
                    mark = jnp.where(lanes // deep == e, base_of(slot, p) + lanes - e * deep, mark)
                marks.append(jnp.broadcast_to(mark.astype(F32), (256, 128)))

        def one(i, carry):
            place = pl.ds(pl.multiple_of(d * rows + i * 256, 256), 256)
            keys = key[place, :]
            got = acc[place, :]
            per = len(marks) // len(slots)
            for n, table in enumerate(tables):
                hot = jnp.concatenate(
                    [jnp.where(keys == mark, 1.0, 0.0).astype(BF16) for mark in marks[n * per : (n + 1) * per]],
                    axis=1,
                )
                both = jnp.dot(hot, table, preferred_element_type=F32)
                got = got + (both[:, :128] + both[:, 128:])
            acc[place, :] = got
            return carry

        lax.fori_loop(0, rows // 256, one, 0)

    def around_sum(ref, r, n):
        mid = ref[pl.ds(r, n)].reshape(n * xe.shape[1], cz)
        out = ref[pl.ds(r - 1, n)] + ref[pl.ds(r + 1, n)]
        out = out.reshape(n * xe.shape[1], cz)
        out = out + (pltpu.roll(mid, 1, 0) + pltpu.roll(mid, mid.shape[0] - 1, 0))
        lane = iota(mid.shape, 1)
        out = out + jnp.where(lane == 0, 0.0, pltpu.roll(mid, 1, 1))
        out = out + jnp.where(lane == cz - 1, 0.0, pltpu.roll(mid, cz - 1, 1))
        return out.reshape(n, xe.shape[1], cz)

    def start_solid():
        for halo in halos:
            halo.wait_recv()
        for ref, fill in ((xe, 0.0), (de, 1e30)):
            @pl.when(f == 0)
            def _():
                ref[pl.ds(LOW - 4, 4)] = jnp.full((4,) + xe.shape[1:], fill, F32)

            @pl.when(f == nf - 1)
            def _():
                ref[pl.ds(LOW + cx, 4)] = jnp.full((4,) + xe.shape[1:], fill, F32)

            @pl.when(s == 0)
            def _():
                ref[pl.ds(1, cx + 8), pl.ds(0, 8)] = jnp.full((cx + 8, 8, cz), fill, F32)

            @pl.when(s == ns - 1)
            def _():
                ref[pl.ds(1, cx + 8), pl.ds(SIDE + cy, 8)] = jnp.full((cx + 8, 8, cz), fill, F32)

        def one(i, carry):
            r = 1 + 8 * i
            got = around_sum(xe, r, 8) - 6.0 * xe[pl.ds(r, 8)]
            c = de[pl.ds(r, 8)]
            inverse = jnp.where(c > 1e29, 0.0, 1.0 / (6.0 + c))
            de[pl.ds(r, 8)] = inverse
            w0[pl.ds(r, 8)] = inverse * got
            return carry

        lax.fori_loop(0, (cx + 8) // 8, one, 0)

    for halo in halos:
        halo.wait_send()
    start_solid()
    for d in range(nx):
        prepare(d)
    for t in range(2, half + 1):
        far = t - 2
        slots = [y] if far == 0 else [lax.rem(y + ny - far, ny), lax.rem(y + far, ny)]
        for d in range(nx):
            forward(t, d)
            pick(d, slots)
    far = half - 1
    slots = [y] if far == 0 else [lax.rem(y + ny - far, ny), lax.rem(y + far, ny)]
    for d in range(nx):
        pick(d, slots)
    for d in range(nx):
        for way in range(2):
            if goes(half, d, way):
                ways[half - 1][d][way].wait_recv()
    for d in range(nx):
        pick(d, [lax.rem(y + half, ny)])

        def one(i, carry):
            place = pl.ds(pl.multiple_of(d * rows + i * 128, 128), 128)
            product = acc[place, :] * jm[place, :]
            part_out[d, pl.ds(i, 1), :] = jnp.sum(product.T, axis=0, keepdims=True)
            return carry

        lax.fori_loop(0, rowsets, one, 0)
    parts = []
    for d in range(1, nx):
        parts.append(
            remote(part_out.at[d], part_in.at[d - 1], px_send.at[d - 1], px_recv.at[d - 1], on_x(nx - d, 0))
        )
        parts[-1].start()
    total = part_out[0]
    for d in range(1, nx):
        parts[d - 1].wait_recv()
    for d in range(1, nx):
        total = total + part_in[d - 1]
    source[...] = total

    shared = []
    for n, (a, b) in enumerate(AROUND):
        shared.append(remote(source, around_in.at[n], sh_send.at[n], sh_recv.at[n], beside(a, b)))
        shared[-1].start()

    def heat(r, first, n, line, offset):
        spot = iota((n, 128), 1)
        column = jnp.where(spot == iota((n, 128), 0) + offset, jnp.broadcast_to(line, (n, 128)), 0.0)
        column = jnp.sum(column, axis=1, keepdims=True)
        w0[r, pl.ds(first, n), :] += jnp.where(spot == cz - 1, column * de[r, pl.ds(first, n), :], 0.0)

    per = 128 // cy

    def heat_inner(i, carry):
        line = source[pl.ds(i, 1), :]
        for k in range(per):
            heat(LOW + i * per + k, SIDE, cy, line, k * cy)
        return carry

    lax.fori_loop(0, cx // per, heat_inner, 0)
    for n, (a, b) in enumerate(AROUND):
        shared[n].wait_recv()
    for n, (a, b) in enumerate(AROUND):
        first = {0: SIDE, 1: 0, -1: SIDE + cy}[b]
        count = {0: cy, 1: 8, -1: 8}[b]
        offset = {0: 0, 1: cy - 8, -1: 0}[b]
        if a == 0:
            def heat_side(i, carry, n=n, first=first, count=count, offset=offset):
                line = around_in[n, pl.ds(i, 1), :]
                for k in range(per):
                    heat(LOW + i * per + k, first, count, line, k * cy + offset)
                return carry

            lax.fori_loop(0, cx // per, heat_side, 0)
        else:
            line = around_in[n, cx // per - 1 : cx // per, :] if a == 1 else around_in[n, 0:1, :]
            for k in range(per):
                heat((1 if a == 1 else LOW + cx) + k, first, count, line, k * cy + offset)

    def fold(v):
        return jnp.sum(v.reshape(-1, 8, cz), axis=0)

    def inside(v):
        return v[:, SIDE : SIDE + cy]

    def step(ref, new, first):
        def one(i, carry):
            r = LOW + 8 * i
            near = around_sum(ref, r, 8)
            inverse = de[pl.ds(r, 8)]
            new_w = inverse * near
            new[pl.ds(r, 8)] = new_w
            now = inside(ref[pl.ds(r, 8)])
            near = inside(near)
            odd = carry[0] + fold(now * near)
            even = carry[1] + fold(inside(new_w) * near)
            if first:
                return (odd, even, carry[2] + fold(now * now / inside(inverse)))
            return (odd, even)

        zero = jnp.zeros((8, cz), F32)
        sums = lax.fori_loop(0, cx // 8, one, (zero,) * (3 if first else 2))
        for r in (LOW - 4, LOW + cx):
            new[pl.ds(r, 4)] = de[pl.ds(r, 4)] * around_sum(ref, r, 4)
        return sums

    mu1, mu2, mu0 = step(w0, w1, True)
    mu3, mu4 = step(w1, w2, False)

    def final(i, carry):
        near = inside(around_sum(w2, LOW + 8 * i, 8))
        last[pl.ds(8 * i, 8)] = near
        return carry + fold(inside(w2[pl.ds(LOW + 8 * i, 8)]) * near)

    mu5 = lax.fori_loop(0, cx // 8, final, jnp.zeros((8, cz), F32))
    lines = [jnp.sum(v, axis=0, keepdims=True) for v in (mu0, mu1, mu2, mu3, mu4, mu5)]
    lines.append(jnp.zeros((2, cz), F32))
    local = jnp.concatenate(lines, axis=0)

    sends = []

    def reduce(stage, value, slots, me, peers):
        sum_out[stage] = value
        slots[me] = value
        copies = []
        for n, at in enumerate(peers):
            copies.append(
                remote(sum_out.at[stage], slots.at[me], ar_send.at[stage, n], ar_recv.at[stage, n], at)
            )
            copies[-1].start()
        for copy in copies:
            copy.wait_recv()
        sends.extend(copies)
        return jnp.sum(slots[...], axis=0)

    local = reduce(0, local, sum_x, x * CORES + core, [on_x(d, flip) for d, flip in plane])
    local = reduce(1, local, sum_y, y, [on_y(d) for d in range(1, ny)])
    local = reduce(2, local, sum_z, z, [on_z(d) for d in range(1, nz)])
    total = jnp.broadcast_to(jnp.sum(local, axis=1, keepdims=True), (8, cz))
    mu = [total[k : k + 1] for k in range(6)]

    def product(u, v):
        out = 0.0
        for a, left in enumerate(u):
            for b, right in enumerate(v):
                out = out + left * right * mu[a + b]
        return out

    one_line = jnp.ones((1, cz), F32)
    course, misfit, guess = [one_line], [one_line], []
    rz = mu[0]
    for it in range(ITERS):
        image = [
            (course[k] if k < len(course) else 0.0) - (course[k - 1] if k > 0 else 0.0)
            for k in range(len(course) + 1)
        ]
        alpha = rz / product(course, image)
        guess = [(guess[k] if k < len(guess) else 0.0) + alpha * course[k] for k in range(len(course))]
        misfit = [(misfit[k] if k < len(misfit) else 0.0) - alpha * image[k] for k in range(len(image))]
        if it + 1 < ITERS:
            new = product(misfit, misfit)
            ratio = new / rz
            course = [misfit[k] + (ratio * course[k] if k < len(course) else 0.0) for k in range(len(misfit))]
            rz = new

    def combine(i, carry):
        here = (pl.ds(LOW + 4 * i, 4), pl.ds(SIDE, cy))
        basis = [w0[here], w1[here], w2[here]]
        step_sum, rest = 0.0, 0.0
        for k in range(3):
            step_sum = step_sum + guess[k] * basis[k]
            rest = rest + misfit[k] * basis[k]
        xe[here] = xe[here] + step_sum
        spot = pl.ds(4 * i, 4)
        last[spot] = rest / de[here] + misfit[3] * last[spot]
        return carry

    lax.fori_loop(0, cx // 4, combine, 0)
    stores = [
        pltpu.make_async_copy(xe.at[inner], guess_hbm, store_sem.at[0]),
        pltpu.make_async_copy(last, misfit_hbm, store_sem.at[1]),
    ]
    for store in stores:
        store.start()
    for copy in spread + coded + jacs + parts + shared + sends:
        copy.wait_send()
    for t in range(1, half + 1):
        for d in range(nx):
            for way in range(2):
                if goes(t, d, way):
                    ways[t - 1][d][way].wait_send()
    for store in stores:
        store.wait()


def per_device(nx, ny, nz, x0, c, b, j, owner, slot):
    quads, faces = b.shape
    rows = slot.shape[0]
    cx, cy, cz = x0.shape
    share = quads // nx
    deep = faces * share // 128
    half = ny // 2
    wide = (cx + 10, cy + 16, cz)
    lines = rows // 128
    dma = pltpu.SemaphoreType.DMA
    vmem = pltpu.VMEM
    peers = max(nx * CORES, ny, nz)
    scratch = [
        vmem(wide, F32), vmem(wide, F32), vmem(wide, F32), vmem(wide, F32), vmem(wide, F32), vmem((cx, cy, cz), F32),
        vmem((quads, faces), F32), vmem((quads, rows), F32), vmem((2, lines, 128), jnp.int32),
        vmem((nx, deep, 128), F32), vmem((ny, nx, deep, 128), F32), vmem((nx, share, rows), F32),
        vmem((nx, lines, 128), jnp.int32), vmem((lines, 128), jnp.int32),
        vmem((nx * rows, 128), F32), vmem((nx * rows, 128), F32), vmem((nx * rows, 128), F32),
        vmem((nx, lines, 128), F32), vmem((nx - 1, lines, 128), F32), vmem((lines, 128), F32),
        vmem((8, lines, 128), F32), vmem((3, 8, 128), F32),
        vmem((nx * CORES, 8, 128), F32), vmem((ny, 8, 128), F32), vmem((nz, 8, 128), F32),
        dma((6,)), dma((2,)), dma((nx - 1,)), dma((nx - 1,)), dma((nx - 1,)), dma((nx - 1,)), dma((nx - 1,)), dma((nx - 1,)),
        dma((2, half, nx)), dma((2, half, nx)), dma((2, 8)), dma((2, 8)), dma((nx - 1,)), dma((nx - 1,)),
        dma((8,)), dma((8,)), dma((3, peers)), dma((3, peers)),
    ]
    out = jax.ShapeDtypeStruct((cx, cy, cz), F32)
    anywhere = pl.BlockSpec(memory_space=pl.ANY)
    return pl.pallas_call(
        functools.partial(body, nx, ny, nz),
        out_shape=(out, out),
        in_specs=[anywhere] * 6,
        out_specs=(anywhere, anywhere),
        scratch_shapes=scratch,
        compiler_params=pltpu.CompilerParams(collective_id=0, has_side_effects=True, vmem_limit_bytes=40 * 2**20),
        name="coupling_step",
    )(x0, c, b, j, owner.reshape(lines, 128), slot.reshape(lines, 128))


def solution(mesh):
    nx, nz = XCHIPS, mesh.shape["solid"] // CORES
    ny = mesh.shape["fluid"] // nx
    both = ("fluid", "solid")
    block = P("fluid", "solid", None)
    return jax.shard_map(
        functools.partial(per_device, nx, ny, nz),
        mesh=mesh,
        in_specs=(block, block, P(None, both), P(None, both), P(both, None), P(both)),
        out_specs=(block, block),
        check_vma=False,
    )
```

time: 310 us -> 84.2 us (0.27)
  blocking collectives: 154 us -> 0 us
  Pallas kernels: 0 us -> 76.3 us
  starting transfers between devices: 65 us -> 0 us
  other arithmetic: 31.3 us -> 0 us
  local copies, waits for them, and re-layouts: 27.3 us -> 6.89 us
  waiting for transfers between devices: 19.6 us -> 0 us
  between operations: 11.1 us -> 0.65 us
    psum x12 -> x0, blocking collectives: 154 us -> none  [by_axis(): shard = lax.psum(shard, axis)]
    pallas_call x0 -> x1, Pallas kernels: none -> 76.3 us  [per_device(): pl.pallas_call(functools.partial(body, nx, ny, nz), out_shape=(out, out),...]
    ppermute x16 -> x0, starting transfers between devices: 49.7 us -> none  [the longest x8 29.6 us: extended(): lax.ppermute(last, axis, up)]
    all_to_all x2 -> x0, waiting for transfers between devices: 17.2 us -> none  [the longest x1 8.82 us: per_device(): lax.all_to_all(rows_out, FLUID, split_axis=1, concat_axis=1, tiled=True)]
    gather x3 -> x0, local copies, waits for them, and re-layouts: 15.3 us -> none  [the longest x2 11.3 us: per_device(): jnp.take(boundary_energy_current, lax.all_to_all(request, FLUID, split_ax...]
    all_to_all x2 -> x0, starting transfers between devices: 15.3 us -> none  [the longest x1 10.5 us: per_device(): lax.all_to_all(request, FLUID, split_axis=0, concat_axis=0, tiled=True)]
    another operation x3 -> x0, other arithmetic: 9.15 us -> none
    reduce_sum x5 -> x0, other arithmetic: 7.29 us -> none  [the longest x3 4.94 us: paired_sums(): jnp.sum(image * precond)]
  transfers between devices with their start and end apart: 18 -> 0, of which waited for: 5 -> 0; matrix products, arithmetic and copies ran while one was open for 1% -> 0% of each run, Pallas kernels for 0% -> 0%
where the time goes in v1:
time: 84.2 us; the launch traced here: 83.9 us
  Pallas kernels  76.3 us (91%)
  local copies, waits for them, and re-layouts  6.89 us (8%)
    pallas_call x1, Pallas kernels, per_device(): pl.pallas_call(functools.partial(body, nx, ny, nz), out_shape=(out, out),...  76.3 us
    unnamed x14, local copies, waits for them, and re-layouts  6.89 us

profile of v1, /device:TPU:1, one launch (start us, length us, event | category | flops | bytes accessed | tf_op | source)
XLA Modules:
  0.0 83.9 jit_solution(14233489175757994623)
XLA Ops:
  0.6 0.0 copy-start
  0.6 1.0 %copy-done = f32[32,32,128]{2,1,0:T(8,128)S(1)} copy-done((f32[32,32,128]{2,1,0:T(8,128)S(1)}, f32[32,32,128]{2,1,0:T(8,128)}, u32[]{:S(2)}) %copy-start) | copy-done | bytes 524312
  1.7 0.0 copy-start.1
  1.7 1.0 %copy-done.1 = f32[32,32,128]{2,1,0:T(8,128)S(1)} copy-done((f32[32,32,128]{2,1,0:T(8,128)S(1)}, f32[32,32,128]{2,1,0:T(8,128)}, u32[]{:S(2)}) %copy-start.1) | copy-done | bytes 524312
  2.7 0.0 copy-start.2
  2.7 0.9 %copy-done.2 = f32[64,1024]{1,0:T(8,128)S(1)} copy-done((f32[64,1024]{1,0:T(8,128)S(1)}, f32[64,1024]{1,0:T(8,128)}, u32[]{:S(2)}) %copy-start.2) | copy-done | bytes 262168
  3.7 0.0 copy-start.3
  3.7 0.9 %copy-done.3 = f32[64,512]{1,0:T(8,128)S(1)} copy-done((f32[64,512]{1,0:T(8,128)S(1)}, f32[64,512]{1,0:T(8,128)}, u32[]{:S(2)}) %copy-start.3) | copy-done | bytes 131096
  4.6 0.0 copy-start.4
  4.6 0.7 copy-done.4
  5.3 0.0 copy-start.5
  5.3 0.7 copy-done.5
  5.9 76.3 %coupling_step.1 = (f32[32,32,128]{2,1,0:T(8,128)S(1)}, f32[32,32,128]{2,1,0:T(8,128)S(1)}) custom-call(f32[32,32,128]{2,1,0:T(8,128)S(1)} %copy-done, f32[32,32,128]{2,1,0:T(8,128)S(1)} %copy-done.1, f32[64,512]{1,0:T(8,128)S(1)} %copy-done.3, f32[64,1024]{1,0:T(8,128)S(1)} %copy-done.2, s32[8,128]{1,0:T(8,128)S(1)} %bitcast.2, s32[8,128]{1,0:T(8,128)S(1)} %bitcast.3), custom_call_target="tpu_custom_call" | custom-call | tf_op jit(solution)/shard_map/coupling_step/pallas_call | solution.py:504
  82.3 0.8 copy.10
  83.1 0.8 copy.11
Async XLA Ops:
  0.6 1.0 %copy-start = (f32[32,32,128]{2,1,0:T(8,128)S(1)}, f32[32,32,128]{2,1,0:T(8,128)}, u32[]{:S(2)}) copy-start(f32[32,32,128]{2,1,0:T(8,128)} %x0_hbm.1) | copy-start | bytes 1572868
  1.7 1.0 %copy-start.1 = (f32[32,32,128]{2,1,0:T(8,128)S(1)}, f32[32,32,128]{2,1,0:T(8,128)}, u32[]{:S(2)}) copy-start(f32[32,32,128]{2,1,0:T(8,128)} %c_hbm.1) | copy-start | bytes 1572868
  2.7 0.9 %copy-start.2 = (f32[64,1024]{1,0:T(8,128)S(1)}, f32[64,1024]{1,0:T(8,128)}, u32[]{:S(2)}) copy-start(f32[64,1024]{1,0:T(8,128)} %j_hbm.1) | copy-start | bytes 786436
  3.7 0.9 %copy-start.3 = (f32[64,512]{1,0:T(8,128)S(1)}, f32[64,512]{1,0:T(8,128)}, u32[]{:S(2)}) copy-start(f32[64,512]{1,0:T(8,128)} %b_hbm.1) | copy-start | bytes 393220
  4.6 0.7 copy-start.4
  5.3 0.7 copy-start.5

commit v2 on v1

v2 whole, which is shorter than its diff:
```python
import functools

import jax
import jax.numpy as jnp
from jax import lax
from jax.experimental import pallas as pl
from jax.experimental.pallas import tpu as pltpu
from jax.sharding import PartitionSpec as P

ITERS = 3
XCHIPS = 4
CORES = 2
MESH = pl.DeviceIdType.MESH
F32 = jnp.float32
BF16 = jnp.bfloat16
AROUND = [(a, b) for a in (-1, 0, 1) for b in (-1, 0, 1) if (a, b) != (0, 0)]
LOW = 5
SIDE = 8


def iota(shape, axis):
    return lax.broadcasted_iota(jnp.int32, shape, axis)


def body(
    nx, ny, nz,
    x0_hbm, c_hbm, b_hbm, j_hbm, owner_hbm, slot_hbm,
    xe, de, w0, w1, w2, last, coefs,
    bv, jv, idx, tabs, held, jac, codes, code_own, key, jm, acc,
    part_out, part_in, source, around_in, sum_out, sum_plane, sum_line,
    load_sem, bx_send, bx_recv, jx_send, jx_recv, cx_send, cx_recv,
    ring_send, ring_recv, halo_send, halo_recv, px_send, px_recv,
    sh_send, sh_recv, ar_send, ar_recv,
):
    cx, cy, cz = (xe.shape[0] - 10, xe.shape[1] - 16, xe.shape[2])
    quads, faces = bv.shape
    rows = jv.shape[1]
    share = quads // nx
    many = 128 // share
    deep = faces // many
    rowsets = rows // 128
    f, s = lax.axis_index("fluid"), lax.axis_index("solid")
    nf, ns = nx * ny, nz * CORES
    x, y = lax.rem(f, nx), f // nx

    def remote(src, dst, send, recv, at):
        return pltpu.make_async_remote_copy(
            src_ref=src, dst_ref=dst, send_sem=send, recv_sem=recv,
            device_id=at, device_id_type=MESH,
        )

    def beside(a, b):
        return (lax.rem(f + a + nf, nf), lax.rem(s + b + ns, ns))

    def on_x(d):
        return (y * nx + lax.rem(x + d, nx), s)

    def on_y(d):
        return (lax.rem(y + d, ny) * nx + x, s)

    def on_plane(n):
        return (lax.rem(f + n, nf), s)

    def on_line(n):
        return (f, lax.rem(s + n, ns))

    inner = (pl.ds(LOW, cx), pl.ds(SIDE, cy))
    loads = [
        pltpu.make_async_copy(b_hbm, bv, load_sem.at[0]),
        pltpu.make_async_copy(owner_hbm, idx.at[0], load_sem.at[1]),
        pltpu.make_async_copy(slot_hbm, idx.at[1], load_sem.at[2]),
        pltpu.make_async_copy(j_hbm, jv, load_sem.at[3]),
        pltpu.make_async_copy(x0_hbm, xe.at[inner], load_sem.at[4]),
        pltpu.make_async_copy(c_hbm, de.at[inner], load_sem.at[5]),
    ]
    for load in loads:
        load.start()

    barrier = pltpu.get_barrier_semaphore()
    partners = [on_x(d) for d in range(1, nx)] + [on_line(n) for n in range(1, ns)]
    partners += [on_y(1), on_y(ny - 1)] + [beside(a, b) for a, b in AROUND if a != 0]
    for at in partners:
        pl.semaphore_signal(barrier, inc=1, device_id=at, device_id_type=MESH)

    guard = jnp.zeros(xe.shape[1:], F32)
    for ref in (xe, w0, w1, w2):
        ref[0] = guard
        ref[cx + 9] = guard

    with jax.named_scope("tables"):
        loads[0].wait()
        for a in range(nx):
            mine = bv[a * share : (a + 1) * share, :]
            stack = jnp.concatenate(
                [mine[:, (m * deep // 128) * 128 : (m * deep // 128) * 128 + 128] for m in range(many)], axis=0
            )
            if deep < 128:
                turned = pltpu.roll(stack, 128 - deep, 1)
                odd = (iota(stack.shape, 0) // share) % 2 == 1
                stack = jnp.where(odd, turned, stack)
            tabs[a] = stack.T[:deep]
        loads[1].wait()
        loads[2].wait()
        code_own[...] = idx[0] * faces + idx[1]
        codes[0] = code_own[...]
        held[y, 0] = tabs[x]
        loads[3].wait()
        jac[0] = jv[pl.ds(pl.multiple_of(x * share, share), share), :]
        loads[4].wait()
        loads[5].wait()

    with jax.named_scope("entry"):
        pl.semaphore_wait(barrier, len(partners))

    spread, coded, jacs, halos = [], [], [], []
    for d in range(1, nx):
        coded.append(remote(code_own, codes.at[d], cx_send.at[d - 1], cx_recv.at[d - 1], on_x(d)))
        coded[-1].start()
    for d in range(1, nx):
        to = lax.rem(x + d, nx)
        spread.append(remote(tabs.at[to], held.at[y, d], bx_send.at[d - 1], bx_recv.at[d - 1], on_x(d)))
        spread[-1].start()

    def ring(t, d, way):
        slot = lax.rem(y + ny + (1 - t if way == 0 else t - 1), ny)
        at = on_y(1 if way == 0 else ny - 1)
        block = held.at[slot, d]
        return remote(block, block, ring_send.at[way, t - 1, d], ring_recv.at[way, t - 1, d], at)

    half = ny // 2

    def goes(t, d, way):
        return t < half or (d < nx // 2) == (way == 0)

    ways = [
        [[ring(t, d, way) if goes(t, d, way) else None for way in range(2)] for d in range(nx)]
        for t in range(1, half + 1)
    ]

    def forward(t, d):
        if t == 1 and d > 0:
            spread[d - 1].wait_recv()
        for way in range(2):
            if t > 1:
                ways[t - 2][d][way].wait_recv()
            if goes(t, d, way):
                ways[t - 1][d][way].start()

    forward(1, 0)
    def prepare_keys(d):
        if d > 0:
            coded[d - 1].wait_recv()
        for i in range(rowsets):
            code = codes[d, i : i + 1, :]
            owner, slot = code // faces, lax.rem(code, faces)
            keys = (owner * deep + lax.rem(slot, deep)).astype(F32)
            key[d * rows + i * 128 : d * rows + (i + 1) * 128, :] = jnp.broadcast_to(keys, (128, 128)).T

    def prepare_jac(d):
        if d > 0:
            jacs[d - 1].wait_recv()
        for i in range(rowsets):
            slot = lax.rem(codes[d, i : i + 1, :], faces)
            j = jac[d, :, i * 128 : (i + 1) * 128]
            tiled = jnp.concatenate([j] * many, axis=0)
            wanted = iota((128, 128), 0) // share == jnp.broadcast_to(slot // deep, (128, 128))
            jm[d * rows + i * 128 : d * rows + (i + 1) * 128, :] = jnp.where(wanted, tiled, 0.0).T

    def weight(slot):
        parts = []
        for d in range(nx):
            parts.append(held[slot, d])
        table = jnp.concatenate(parts, axis=0)
        high = table.astype(BF16)
        low = (table - high.astype(F32)).astype(BF16)
        return jnp.concatenate([high, low], axis=1)

    def base_of(slot, d):
        return (slot * nx + lax.rem(x - d + nx, nx)) * deep

    tall = 512

    def pick(d, slots, first=False, finish=False):
        table = jnp.concatenate([weight(slot) for slot in slots], axis=0)
        lanes = iota((1, 128), 1)
        marks = []
        for slot in slots:
            for tile in range(nx * deep // 128):
                mark = jnp.zeros((1, 128), jnp.int32)
                for e in range(128 // deep):
                    p = tile * (128 // deep) + e
                    mark = jnp.where(lanes // deep == e, base_of(slot, p) + lanes - e * deep, mark)
                marks.append(mark.astype(F32))
        for i in range(rows // tall):
            place = pl.ds(d * rows + i * tall, tall)
            keys = key[place, :]
            hot = jnp.concatenate([jnp.where(keys == mark, 1.0, 0.0).astype(BF16) for mark in marks], axis=1)
            both = jnp.dot(hot, table, preferred_element_type=F32)
            got = both[:, :128] + both[:, 128:]
            if not first:
                got = got + acc[place, :]
            if not finish:
                acc[place, :] = got
                continue
            product = got * jm[place, :]
            for k in range(tall // 128):
                line = jnp.sum(product[k * 128 : (k + 1) * 128].T, axis=0, keepdims=True)
                at = i * (tall // 128) + k
                part_out[d, at : at + 1, :] = line

    def around_sum(ref, r, n):
        mid = ref[pl.ds(r, n)].reshape(n * xe.shape[1], cz)
        out = ref[pl.ds(r - 1, n)] + ref[pl.ds(r + 1, n)]
        out = out.reshape(n * xe.shape[1], cz)
        out = out + (pltpu.roll(mid, 1, 0) + pltpu.roll(mid, mid.shape[0] - 1, 0))
        lane = iota(mid.shape, 1)
        out = out + jnp.where(lane == 0, 0.0, pltpu.roll(mid, 1, 1))
        out = out + jnp.where(lane == cz - 1, 0.0, pltpu.roll(mid, cz - 1, 1))
        return out.reshape(n, xe.shape[1], cz)

    def start_solid():
        for ref, fill in ((xe, 0.0), (de, 1e30)):
            @pl.when(f == 0)
            def _():
                ref[pl.ds(LOW - 4, 4)] = jnp.full((4,) + xe.shape[1:], fill, F32)

            @pl.when(f == nf - 1)
            def _():
                ref[pl.ds(LOW + cx, 4)] = jnp.full((4,) + xe.shape[1:], fill, F32)

            @pl.when(s == 0)
            def _():
                ref[pl.ds(1, cx + 8), pl.ds(0, 8)] = jnp.full((cx + 8, 8, cz), fill, F32)

            @pl.when(s == ns - 1)
            def _():
                ref[pl.ds(1, cx + 8), pl.ds(SIDE + cy, 8)] = jnp.full((cx + 8, 8, cz), fill, F32)

        def one(i, carry):
            r = 1 + 8 * i
            got = around_sum(xe, r, 8) - 6.0 * xe[pl.ds(r, 8)]
            c = de[pl.ds(r, 8)]
            inverse = jnp.where(c > 1e29, 0.0, 1.0 / (6.0 + c))
            de[pl.ds(r, 8)] = inverse
            w0[pl.ds(r, 8)] = inverse * got
            return carry

        lax.fori_loop(0, (cx + 8) // 8, one, 0)

    order = sorted(range(nx), key=lambda d: (min(d, nx - d), -d))
    for d in order:
        if d > 0:
            with jax.named_scope(f"forward#t=1#d={d}"):
                forward(1, d)
        with jax.named_scope(f"prepare_keys#d={d}"):
            prepare_keys(d)

    for d in range(1, nx):
        to = lax.rem(x + d, nx)
        jacs.append(
            remote(
                jv.at[pl.ds(pl.multiple_of(to * share, share), share)], jac.at[d],
                jx_send.at[d - 1], jx_recv.at[d - 1], on_x(d),
            )
        )
        jacs[-1].start()
    to_x = {-1: (pl.ds(LOW, 4), pl.ds(LOW + cx, 4)), 0: (pl.ds(LOW, cx),) * 2, 1: (pl.ds(LOW + cx - 4, 4), pl.ds(LOW - 4, 4))}
    to_y = {-1: (pl.ds(SIDE, 8), pl.ds(SIDE + cy, 8)), 0: (pl.ds(SIDE, cy),) * 2, 1: (pl.ds(SIDE + cy - 8, 8), pl.ds(SIDE - 8, 8))}
    def send_halos(chosen):
        for n in chosen:
            a, b = AROUND[n]
            for k, ref in enumerate((xe, de)):
                halos.append(
                    remote(
                        ref.at[to_x[a][0], to_y[b][0]], ref.at[to_x[a][1], to_y[b][1]],
                        halo_send.at[k, n], halo_recv.at[k, n], beside(a, b),
                    )
                )
                halos[-1].start()

    send_halos([n for n, (a, b) in enumerate(AROUND) if a == 0])

    def near(far):
        if far == 0:
            return [y]
        return [lax.rem(y + ny - far, ny), lax.rem(y + far, ny)]

    for t in range(2, half + 1):
        for d in order:
            with jax.named_scope(f"forward#t={t}#d={d}"):
                forward(t, d)
            with jax.named_scope(f"pick#t={t}#d={d}"):
                pick(d, near(t - 2), first=t == 2)
            if t == half:
                with jax.named_scope(f"prepare_jac#d={d}"):
                    prepare_jac(d)
    send_halos([n for n, (a, b) in enumerate(AROUND) if a != 0])
    if half == 1:
        for d in range(nx):
            prepare_jac(d)
    for d in range(nx):
        with jax.named_scope(f"pick_near#d={d}"):
            pick(d, near(half - 1), first=half == 1)
    with jax.named_scope("far_wait"):
        for d in range(nx):
            for way in range(2):
                if goes(half, d, way):
                    ways[half - 1][d][way].wait_recv()
    parts = {}
    for d in list(range(1, nx)) + [0]:
        with jax.named_scope(f"pick_far#d={d}"):
            pick(d, [lax.rem(y + half, ny)], finish=True)
        if d > 0:
            parts[d] = remote(part_out.at[d], part_in.at[d - 1], px_send.at[d - 1], px_recv.at[d - 1], on_x(nx - d))
            parts[d].start()
    with jax.named_scope("solid_wait"):
        for halo in halos:
            halo.wait_send()
        for halo in halos:
            halo.wait_recv()
    with jax.named_scope("solid_start"):
        start_solid()
    total = part_out[0]
    with jax.named_scope("part_wait"):
        for d in range(1, nx):
            parts[d].wait_recv()
    for d in range(1, nx):
        total = total + part_in[d - 1]
    source[...] = total

    shared = []
    for n, (a, b) in enumerate(AROUND):
        shared.append(remote(source, around_in.at[n], sh_send.at[n], sh_recv.at[n], beside(a, b)))
        shared[-1].start()

    per = 128 // cy

    def heat(r, first, count, line, offset):
        shape = (per, count, 128)
        spot = iota(shape, 2)
        picked = jnp.where(spot == iota(shape, 0) * cy + iota(shape, 1) + offset, line.reshape(1, 1, 128), 0.0)
        column = jnp.sum(picked, axis=2, keepdims=True)
        here = (pl.ds(r, per), pl.ds(first, count))
        w0[here] = w0[here] + jnp.where(spot == cz - 1, column * de[here], 0.0)

    with jax.named_scope("heat_inner"):
        for i in range(cx // per):
            heat(LOW + i * per, SIDE, cy, source[i : i + 1, :], 0)
    with jax.named_scope("around_wait"):
        for n in range(len(AROUND)):
            shared[n].wait_recv()
    with jax.named_scope("heat_sides"):
        for n, (a, b) in enumerate(AROUND):
            first = {0: SIDE, 1: 0, -1: SIDE + cy}[b]
            count = {0: cy, 1: 8, -1: 8}[b]
            offset = {0: 0, 1: cy - 8, -1: 0}[b]
            spots = {0: range(cx // per), 1: [cx // per - 1], -1: [0]}[a]
            for i in spots:
                r = {0: LOW + i * per, 1: 1, -1: LOW + cx}[a]
                heat(r, first, count, around_in[n, i : i + 1, :], offset)

    def fold(v):
        return jnp.sum(v.reshape(-1, 8, cz), axis=0)

    def inside(v):
        return v[:, SIDE : SIDE + cy]

    def step(ref, new, first):
        def one(i, carry):
            r = LOW + 8 * i
            near = around_sum(ref, r, 8)
            inverse = de[pl.ds(r, 8)]
            new_w = inverse * near
            new[pl.ds(r, 8)] = new_w
            now = inside(ref[pl.ds(r, 8)])
            near = inside(near)
            odd = carry[0] + fold(now * near)
            even = carry[1] + fold(inside(new_w) * near)
            if first:
                return (odd, even, carry[2] + fold(now * now / inside(inverse)))
            return (odd, even)

        zero = jnp.zeros((8, cz), F32)
        sums = lax.fori_loop(0, cx // 8, one, (zero,) * (3 if first else 2))
        for r in (LOW - 4, LOW + cx):
            new[pl.ds(r, 4)] = de[pl.ds(r, 4)] * around_sum(ref, r, 4)
        return sums

    with jax.named_scope("step#k=0"):
        mu1, mu2, mu0 = step(w0, w1, True)
    with jax.named_scope("step#k=1"):
        mu3, mu4 = step(w1, w2, False)

    def final(i, carry):
        near = inside(around_sum(w2, LOW + 8 * i, 8))
        last[pl.ds(8 * i, 8)] = near
        return carry + fold(inside(w2[pl.ds(LOW + 8 * i, 8)]) * near)

    with jax.named_scope("step#k=2"):
        mu5 = lax.fori_loop(0, cx // 8, final, jnp.zeros((8, cz), F32))
    lines = [jnp.sum(v, axis=0, keepdims=True) for v in (mu0, mu1, mu2, mu3, mu4, mu5)]
    lines.append(jnp.zeros((2, cz), F32))
    sums = jnp.sum(jnp.concatenate(lines, axis=0), axis=1, keepdims=True)
    local = jnp.sum(jnp.where(iota((8, 128), 0) == iota((8, 128), 1), sums, 0.0), axis=0, keepdims=True)
    sends = []

    def reduce(stage, value, slots, me, peers):
        sum_out[stage] = value
        slots[me] = value
        for at in peers:
            remote(sum_out.at[stage], slots.at[me], ar_send.at[stage], ar_recv.at[stage], at).start()
        every = slots.at[pl.ds(0, len(peers))]
        everyone = remote(every, every, ar_send.at[stage], ar_recv.at[stage], peers[0])
        everyone.wait_recv()
        sends.append(everyone)
        return jnp.sum(slots[...], axis=0)

    with jax.named_scope("reduce#k=0"):
        local = reduce(0, local, sum_plane, f, [on_plane(n) for n in range(1, nf)])
    with jax.named_scope("reduce#k=1"):
        local = reduce(1, local, sum_line, s, [on_line(n) for n in range(1, ns)])
    lane = iota((1, 128), 1)
    mu = [jnp.sum(jnp.where(lane == k, local, 0.0), axis=1, keepdims=True) for k in range(6)]
    mu = [jnp.broadcast_to(m, (1, 128)) for m in mu]

    def product(u, v):
        out = 0.0
        for a, left in enumerate(u):
            for b, right in enumerate(v):
                out = out + left * right * mu[a + b]
        return out

    one_line = jnp.ones((1, cz), F32)
    course, misfit, guess = [one_line], [one_line], []
    rz = mu[0]
    for it in range(ITERS):
        image = [
            (course[k] if k < len(course) else 0.0) - (course[k - 1] if k > 0 else 0.0)
            for k in range(len(course) + 1)
        ]
        alpha = rz / product(course, image)
        guess = [(guess[k] if k < len(guess) else 0.0) + alpha * course[k] for k in range(len(course))]
        misfit = [(misfit[k] if k < len(misfit) else 0.0) - alpha * image[k] for k in range(len(image))]
        if it + 1 < ITERS:
            new = product(misfit, misfit)
            ratio = new / rz
            course = [misfit[k] + (ratio * course[k] if k < len(course) else 0.0) for k in range(len(misfit))]
            rz = new

    coefs[...] = jnp.concatenate(guess + misfit + [one_line], axis=0)
    with jax.named_scope("sent"):
        for copy in spread + coded + jacs + list(parts.values()) + shared + sends:
            copy.wait_send()
        for t in range(1, half + 1):
            for d in range(nx):
                for way in range(2):
                    if goes(t, d, way):
                        ways[t - 1][d][way].wait_send()


def finish(xe, de, w0, w1, w2, last, coefs, guess, misfit):
    n, cy, _ = guess.shape
    first = pl.program_id(0) * n
    here = (pl.ds(LOW + first, n), pl.ds(SIDE, cy))
    line = [coefs[k : k + 1, :] for k in range(7)]
    basis = [w0[here], w1[here], w2[here]]
    guess[...] = xe[here] + (line[0] * basis[0] + (line[1] * basis[1] + line[2] * basis[2]))
    rest = line[3] * basis[0] + (line[4] * basis[1] + line[5] * basis[2])
    misfit[...] = rest / de[here] + line[6] * last[pl.ds(first, n)]


def per_device(nx, ny, nz, x0, c, b, j, owner, slot):
    quads, faces = b.shape
    rows = slot.shape[0]
    cx, cy, cz = x0.shape
    share = quads // nx
    deep = faces * share // 128
    half = ny // 2
    wide = (cx + 10, cy + 16, cz)
    lines = rows // 128
    nf, ns = nx * ny, nz * CORES
    dma = pltpu.SemaphoreType.DMA
    vmem = pltpu.VMEM
    scratch = [
        vmem((quads, faces), F32), vmem((quads, rows), F32), vmem((2, lines, 128), jnp.int32),
        vmem((nx, deep, 128), F32), vmem((ny, nx, deep, 128), F32), vmem((nx, share, rows), F32),
        vmem((nx, lines, 128), jnp.int32), vmem((lines, 128), jnp.int32),
        vmem((nx * rows, 128), F32), vmem((nx * rows, 128), F32), vmem((nx * rows, 128), F32),
        vmem((nx, lines, 128), F32), vmem((nx - 1, lines, 128), F32), vmem((lines, 128), F32),
        vmem((8, lines, 128), F32), vmem((2, 1, 128), F32), vmem((nf, 1, 128), F32), vmem((ns, 1, 128), F32),
        dma((6,)), dma((nx - 1,)), dma((nx - 1,)), dma((nx - 1,)), dma((nx - 1,)), dma((nx - 1,)), dma((nx - 1,)),
        dma((2, half, nx)), dma((2, half, nx)), dma((2, 8)), dma((2, 8)), dma((nx - 1,)), dma((nx - 1,)),
        dma((8,)), dma((8,)), dma((2,)), dma((2,)),
    ]
    wide_out = jax.ShapeDtypeStruct(wide, F32)
    out = jax.ShapeDtypeStruct((cx, cy, cz), F32)
    whole = pl.BlockSpec(memory_space=vmem)
    operands = (x0, c, b, j, owner.reshape(lines, 128), slot.reshape(lines, 128))
    state = pl.pallas_call(
        functools.partial(body, nx, ny, nz),
        out_shape=(wide_out,) * 5 + (out, jax.ShapeDtypeStruct((8, 128), F32)),
        in_specs=[pl.BlockSpec(memory_space=pltpu.HBM)] * 6,
        out_specs=(whole,) * 7,
        scratch_shapes=scratch,
        compiler_params=pltpu.CompilerParams(collective_id=0, has_side_effects=True, vmem_limit_bytes=44 * 2**20),
        name="coupling_step",
    )(*[pltpu.with_memory_space_constraint(v, pltpu.HBM) for v in operands])
    chunk = pl.BlockSpec((8, cy, cz), lambda i: (i, 0, 0))
    return pl.pallas_call(
        finish,
        grid=(cx // 8,),
        out_shape=(out, out),
        in_specs=[whole] * 7,
        out_specs=(chunk, chunk),
        compiler_params=pltpu.CompilerParams(vmem_limit_bytes=16 * 2**20),
        name="finish_step",
    )(*state)


def solution(mesh):
    nx, nz = XCHIPS, mesh.shape["solid"] // CORES
    ny = mesh.shape["fluid"] // nx
    both = ("fluid", "solid")
    block = P("fluid", "solid", None)
    return jax.shard_map(
        functools.partial(per_device, nx, ny, nz),
        mesh=mesh,
        in_specs=(block, block, P(None, both), P(None, both), P(both, None), P(both)),
        out_specs=(block, block),
        check_vma=False,
    )
```

time: 84.2 us -> 58.7 us (0.70)
  Pallas kernels: 76.3 us -> 57.9 us
  local copies, waits for them, and re-layouts: 6.89 us -> 0 us
    pallas_call x1 -> x2, Pallas kernels: 76.3 us -> 57.9 us  [the longest x1 56.3 us: per_device(): pl.pallas_call(functools.partial(body, nx, ny, nz), out_shape=(wide_out,)...]
    unnamed x14 -> x0, local copies, waits for them, and re-layouts: 6.89 us -> none
where the time goes in v2:
time: 58.7 us; the launch traced here: 58.5 us
  Pallas kernels  57.9 us (99%)
  between operations  0.64 us (1%)
    pallas_call x1, Pallas kernels, per_device(): pl.pallas_call(functools.partial(body, nx, ny, nz), out_shape=(wide_out,)...  56.3 us
    pallas_call x1, Pallas kernels, per_device(): pl.pallas_call(finish, grid=(cx // 8,), out_shape=(out, out), in_specs=[w...  1.59 us

profile of v2, /device:TPU:1, one launch (start us, length us, event | category | flops | bytes accessed | tf_op | source)
XLA Modules:
  0.0 58.5 jit_solution(7564756409260044604)
XLA Ops:
  0.6 56.3 %coupling_step.1 = (f32[42,48,128]{2,1,0:T(8,128)S(1)}, f32[42,48,128]{2,1,0:T(8,128)S(1)}, f32[42,48,128]{2,1,0:T(8,128)S(1)}, f32[42,48,128]{2,1,0:T(8,128)S(1...) custom-call(f32[32,32,128]{2,1,0:T(8,128)} %x0_hbm.1, f32[32,32,128]{2,1,0:T(8,128)} %c_hbm.1, ...), custom_call_target="tpu_custom_call" | custom-call | tf_op jit(solution)/shard_map/coupling_step/pallas_call | solution.py:499
  56.9 1.6 %finish_step.1 = (f32[32,32,128]{2,1,0:T(8,128)}, f32[32,32,128]{2,1,0:T(8,128)}) custom-call(f32[42,48,128]{2,1,0:T(8,128)S(1)} %get-tuple-element.9.xe, f32[42,48,128]{2,1,0:T(8,128)S(1)} %get-tuple-element.10.de, f32[42,48,128]{2,1,0:T(8,128)S(1)} %get-tuple-element.11.w0, f32[42,48,128]{2,1,0:T(8,128)S(1)} %get-tuple-element.12.w1, ...), custom_call_target="tpu_custom_call" | custom-call | tf_op jit(solution)/shard_map/finish_step/pallas_call | solution.py:509

commit v3 on v2

--- a/solution.py
+++ b/solution.py
@@ -25,13 +25,13 @@
 def body(
     nx, ny, nz,
     x0_hbm, c_hbm, b_hbm, j_hbm, owner_hbm, slot_hbm,
-    xe, de, w0, w1, w2, last, coefs,
+    field, w0, w1, w2, last, coefs,
     bv, jv, idx, tabs, held, jac, codes, code_own, key, jm, acc,
-    part_out, part_in, source, around_in, sum_out, sum_plane, sum_line,
+    part_out, part_in, cross_in, edge, sum_out, sum_plane, sum_line,
     load_sem, bx_send, bx_recv, jx_send, jx_recv, cx_send, cx_recv,
-    ring_send, ring_recv, halo_send, halo_recv, px_send, px_recv,
-    sh_send, sh_recv, ar_send, ar_recv,
+    ring_send, ring_recv, halo_send, halo_recv, row_send, row_recv, cross_send, cross_recv, ar_send, ar_recv,
 ):
+    xe, de = field.at[0], field.at[1]
     cx, cy, cz = (xe.shape[0] - 10, xe.shape[1] - 16, xe.shape[2])
     quads, faces = bv.shape
     rows = jv.shape[1]
@@ -57,6 +57,9 @@
 
     def on_y(d):
         return (lax.rem(y + d, ny) * nx + x, s)
+
+    def in_row(a, d, b):
+        return (lax.rem(y + a + ny, ny) * nx + lax.rem(x + d, nx), lax.rem(s + b + ns, ns))
 
     def on_plane(n):
         return (lax.rem(f + n, nf), s)
@@ -78,9 +81,22 @@
 
     barrier = pltpu.get_barrier_semaphore()
     partners = [on_x(d) for d in range(1, nx)] + [on_line(n) for n in range(1, ns)]
+    partners += [in_row(0, d, b) for d in range(1, nx) for b in (-1, 1)]
     partners += [on_y(1), on_y(ny - 1)] + [beside(a, b) for a, b in AROUND if a != 0]
     for at in partners:
         pl.semaphore_signal(barrier, inc=1, device_id=at, device_id_type=MESH)
+
+    @pl.when(x == 0)
+    def _():
+        for b in (-1, 0, 1):
+            for d in range(nx):
+                pl.semaphore_signal(barrier, inc=1, device_id=in_row(-1, d, b), device_id_type=MESH)
+
+    @pl.when(x == nx - 1)
+    def _():
+        for b in (-1, 0, 1):
+            for d in range(nx):
+                pl.semaphore_signal(barrier, inc=1, device_id=in_row(1, d, b), device_id_type=MESH)
 
     guard = jnp.zeros(xe.shape[1:], F32)
     for ref in (xe, w0, w1, w2):
@@ -110,22 +126,26 @@
         loads[5].wait()
 
     with jax.named_scope("entry"):
-        pl.semaphore_wait(barrier, len(partners))
-
-    spread, coded, jacs, halos = [], [], [], []
+        pl.semaphore_wait(barrier, len(partners) + 6)
+
+    spread = []
     for d in range(1, nx):
-        coded.append(remote(code_own, codes.at[d], cx_send.at[d - 1], cx_recv.at[d - 1], on_x(d)))
-        coded[-1].start()
+        remote(code_own, codes.at[d], cx_send, cx_recv, on_x(d)).start()
+    some = pl.ds(0, nx - 1)
+    coded = remote(codes.at[some], codes.at[some], cx_send, cx_recv, on_x(1))
+    jacs = remote(jac.at[some], jac.at[some], jx_send, jx_recv, on_x(1))
+    spread_all = remote(tabs.at[some], tabs.at[some], bx_send, bx_recv.at[0], on_x(1))
+    ring_all = remote(held.at[pl.ds(0, ny - 1)], held.at[pl.ds(0, ny - 1)], ring_send, bx_recv.at[0], on_x(1))
     for d in range(1, nx):
         to = lax.rem(x + d, nx)
-        spread.append(remote(tabs.at[to], held.at[y, d], bx_send.at[d - 1], bx_recv.at[d - 1], on_x(d)))
+        spread.append(remote(tabs.at[to], held.at[y, d], bx_send, bx_recv.at[d - 1], on_x(d)))
         spread[-1].start()
 
     def ring(t, d, way):
         slot = lax.rem(y + ny + (1 - t if way == 0 else t - 1), ny)
         at = on_y(1 if way == 0 else ny - 1)
         block = held.at[slot, d]
-        return remote(block, block, ring_send.at[way, t - 1, d], ring_recv.at[way, t - 1, d], at)
+        return remote(block, block, ring_send, ring_recv.at[way, t - 1, d], at)
 
     half = ny // 2
 
@@ -148,8 +168,6 @@
 
     forward(1, 0)
     def prepare_keys(d):
-        if d > 0:
-            coded[d - 1].wait_recv()
         for i in range(rowsets):
             code = codes[d, i : i + 1, :]
             owner, slot = code // faces, lax.rem(code, faces)
@@ -157,8 +175,6 @@
             key[d * rows + i * 128 : d * rows + (i + 1) * 128, :] = jnp.broadcast_to(keys, (128, 128)).T
 
     def prepare_jac(d):
-        if d > 0:
-            jacs[d - 1].wait_recv()
         for i in range(rowsets):
             slot = lax.rem(codes[d, i : i + 1, :], faces)
             j = jac[d, :, i * 128 : (i + 1) * 128]
@@ -206,7 +222,7 @@
             for k in range(tall // 128):
                 line = jnp.sum(product[k * 128 : (k + 1) * 128].T, axis=0, keepdims=True)
                 at = i * (tall // 128) + k
-                part_out[d, at : at + 1, :] = line
+                part_out[lax.rem(x - d + nx, nx), pl.ds(at, 1), :] = line
 
     def around_sum(ref, r, n):
         mid = ref[pl.ds(r, n)].reshape(n * xe.shape[1], cz)
@@ -249,6 +265,8 @@
 
     order = sorted(range(nx), key=lambda d: (min(d, nx - d), -d))
     for d in order:
+        if d == order[1]:
+            coded.wait_recv()
         if d > 0:
             with jax.named_scope(f"forward#t=1#d={d}"):
                 forward(1, d)
@@ -257,28 +275,30 @@
 
     for d in range(1, nx):
         to = lax.rem(x + d, nx)
-        jacs.append(
-            remote(
-                jv.at[pl.ds(pl.multiple_of(to * share, share), share)], jac.at[d],
-                jx_send.at[d - 1], jx_recv.at[d - 1], on_x(d),
-            )
-        )
-        jacs[-1].start()
+        remote(
+            jv.at[pl.ds(pl.multiple_of(to * share, share), share)], jac.at[d], jx_send, jx_recv, on_x(d)
+        ).start()
     to_x = {-1: (pl.ds(LOW, 4), pl.ds(LOW + cx, 4)), 0: (pl.ds(LOW, cx),) * 2, 1: (pl.ds(LOW + cx - 4, 4), pl.ds(LOW - 4, 4))}
     to_y = {-1: (pl.ds(SIDE, 8), pl.ds(SIDE + cy, 8)), 0: (pl.ds(SIDE, cy),) * 2, 1: (pl.ds(SIDE + cy - 8, 8), pl.ds(SIDE - 8, 8))}
-    def send_halos(chosen):
-        for n in chosen:
-            a, b = AROUND[n]
-            for k, ref in enumerate((xe, de)):
-                halos.append(
-                    remote(
-                        ref.at[to_x[a][0], to_y[b][0]], ref.at[to_x[a][1], to_y[b][1]],
-                        halo_send.at[k, n], halo_recv.at[k, n], beside(a, b),
-                    )
-                )
-                halos[-1].start()
-
-    send_halos([n for n, (a, b) in enumerate(AROUND) if a == 0])
+    def group(a, b):
+        return 0 if a == 0 else 1 if b == 0 else 2
+
+    def send_halos(groups):
+        for a, b in AROUND:
+            k = group(a, b)
+            if k in groups:
+                remote(
+                    field.at[:, to_x[a][0], to_y[b][0]], field.at[:, to_x[a][1], to_y[b][1]],
+                    halo_send.at[k], halo_recv.at[k], beside(a, b),
+                ).start()
+
+    rims = [
+        field.at[:, pl.ds(LOW, cx), pl.ds(0, 16)],
+        field.at[:, pl.ds(LOW - 4, 8), pl.ds(SIDE, cy)],
+        field.at[:, pl.ds(LOW - 4, 8), pl.ds(0, 16)],
+    ]
+    halos = [remote(rim, rim, halo_send.at[k], halo_recv.at[k], on_x(1)) for k, rim in enumerate(rims)]
+    send_halos((0,))
 
     def near(far):
         if far == 0:
@@ -292,10 +312,13 @@
             with jax.named_scope(f"pick#t={t}#d={d}"):
                 pick(d, near(t - 2), first=t == 2)
             if t == half:
+                if d == 0:
+                    jacs.wait_recv()
                 with jax.named_scope(f"prepare_jac#d={d}"):
                     prepare_jac(d)
-    send_halos([n for n, (a, b) in enumerate(AROUND) if a != 0])
+    send_halos((1, 2))
     if half == 1:
+        jacs.wait_recv()
         for d in range(nx):
             prepare_jac(d)
     for d in range(nx):
@@ -306,13 +329,22 @@
             for way in range(2):
                 if goes(half, d, way):
                     ways[half - 1][d][way].wait_recv()
-    parts = {}
-    for d in list(range(1, nx)) + [0]:
+    for d in range(nx):
         with jax.named_scope(f"pick_far#d={d}"):
             pick(d, [lax.rem(y + half, ny)], finish=True)
-        if d > 0:
-            parts[d] = remote(part_out.at[d], part_in.at[d - 1], px_send.at[d - 1], px_recv.at[d - 1], on_x(nx - d))
-            parts[d].start()
+
+    part_in[nx + x] = part_out[...]
+    for b in (-1, 0, 1):
+        slot = (1 - b) * nx + x
+        remote(part_out.at[nx - 1], cross_in.at[0, slot], cross_send, cross_recv.at[0], in_row(1, nx - x, b)).start()
+        remote(part_out.at[0], cross_in.at[1, slot], cross_send, cross_recv.at[1], in_row(-1, 2 * nx - 1 - x, b)).start()
+        for d in range(nx):
+            if (d, b) != (0, 0):
+                remote(part_out, part_in.at[slot], row_send, row_recv, in_row(0, d, b)).start()
+    most = part_in.at[pl.ds(0, 3 * nx - 1)]
+    rows_all = remote(most, most, row_send, row_recv, on_x(1))
+    six = cross_in.at[0, pl.ds(0, 6)]
+    cross_all = remote(six, six, cross_send, cross_recv.at[0], on_x(1))
     with jax.named_scope("solid_wait"):
         for halo in halos:
             halo.wait_send()
@@ -320,18 +352,13 @@
             halo.wait_recv()
     with jax.named_scope("solid_start"):
         start_solid()
-    total = part_out[0]
     with jax.named_scope("part_wait"):
-        for d in range(1, nx):
-            parts[d].wait_recv()
-    for d in range(1, nx):
-        total = total + part_in[d - 1]
-    source[...] = total
-
-    shared = []
-    for n, (a, b) in enumerate(AROUND):
-        shared.append(remote(source, around_in.at[n], sh_send.at[n], sh_recv.at[n], beside(a, b)))
-        shared[-1].start()
+        rows_all.wait_recv()
+        for side, end in ((0, 0), (1, nx - 1)):
+            @pl.when(x == end)
+            def _():
+                whole = cross_in.at[side]
+                remote(whole, whole, cross_send, cross_recv.at[side], on_x(1)).wait_recv()
 
     per = 128 // cy
 
@@ -343,21 +370,34 @@
         here = (pl.ds(r, per), pl.ds(first, count))
         w0[here] = w0[here] + jnp.where(spot == cz - 1, column * de[here], 0.0)
 
-    with jax.named_scope("heat_inner"):
-        for i in range(cx // per):
-            heat(LOW + i * per, SIDE, cy, source[i : i + 1, :], 0)
-    with jax.named_scope("around_wait"):
-        for n in range(len(AROUND)):
-            shared[n].wait_recv()
-    with jax.named_scope("heat_sides"):
-        for n, (a, b) in enumerate(AROUND):
-            first = {0: SIDE, 1: 0, -1: SIDE + cy}[b]
-            count = {0: cy, 1: 8, -1: 8}[b]
-            offset = {0: 0, 1: cy - 8, -1: 0}[b]
-            spots = {0: range(cx // per), 1: [cx // per - 1], -1: [0]}[a]
-            for i in spots:
-                r = {0: LOW + i * per, 1: 1, -1: LOW + cx}[a]
-                heat(r, first, count, around_in[n, i : i + 1, :], offset)
+    def gathered(b, reader, spots):
+        return sum(part_in[(b + 1) * nx + h, reader, spots, :] for h in range(nx))
+
+    with jax.named_scope("heat"):
+        for a, end, side, spot in ((1, nx - 1, 1, 0), (-1, 0, 0, cx // per - 1)):
+            for b in (-1, 0, 1):
+                here = pl.ds(3 * side + b + 1, 1)
+
+                @pl.when(x == end)
+                def _():
+                    edge[here, :] = sum(cross_in[side, (b + 1) * nx + h, spot : spot + 1, :] for h in range(nx))
+
+                @pl.when(x != end)
+                def _():
+                    edge[here, :] = gathered(b, lax.rem(x + a + nx, nx), slice(spot, spot + 1))
+
+        for a in (-1, 0, 1):
+            for b in (-1, 0, 1):
+                first = {0: SIDE, -1: 0, 1: SIDE + cy}[b]
+                count = {0: cy, -1: 8, 1: 8}[b]
+                offset = {0: 0, -1: cy - 8, 1: 0}[b]
+                if a == 0:
+                    block = gathered(b, x, slice(0, cx // per))
+                    for i in range(cx // per):
+                        heat(LOW + i * per, first, count, block[i : i + 1], offset)
+                else:
+                    at = 3 * (1 if a == 1 else 0) + b + 1
+                    heat(LOW + cx if a == 1 else LOW - 4, first, count, edge[at : at + 1, :], offset)
 
     def fold(v):
         return jnp.sum(v.reshape(-1, 8, cz), axis=0)
@@ -449,16 +489,12 @@
 
     coefs[...] = jnp.concatenate(guess + misfit + [one_line], axis=0)
     with jax.named_scope("sent"):
-        for copy in spread + coded + jacs + list(parts.values()) + shared + sends:
+        for copy in [spread_all, coded, jacs, ring_all, rows_all, cross_all] + sends:
             copy.wait_send()
-        for t in range(1, half + 1):
-            for d in range(nx):
-                for way in range(2):
-                    if goes(t, d, way):
-                        ways[t - 1][d][way].wait_send()
-
-
-def finish(xe, de, w0, w1, w2, last, coefs, guess, misfit):
+
+
+def finish(field, w0, w1, w2, last, coefs, guess, misfit):
+    xe, de = field.at[0], field.at[1]
     n, cy, _ = guess.shape
     first = pl.program_id(0) * n
     here = (pl.ds(LOW + first, n), pl.ds(SIDE, cy))
@@ -486,11 +522,10 @@
         vmem((nx, deep, 128), F32), vmem((ny, nx, deep, 128), F32), vmem((nx, share, rows), F32),
         vmem((nx, lines, 128), jnp.int32), vmem((lines, 128), jnp.int32),
         vmem((nx * rows, 128), F32), vmem((nx * rows, 128), F32), vmem((nx * rows, 128), F32),
-        vmem((nx, lines, 128), F32), vmem((nx - 1, lines, 128), F32), vmem((lines, 128), F32),
-        vmem((8, lines, 128), F32), vmem((2, 1, 128), F32), vmem((nf, 1, 128), F32), vmem((ns, 1, 128), F32),
-        dma((6,)), dma((nx - 1,)), dma((nx - 1,)), dma((nx - 1,)), dma((nx - 1,)), dma((nx - 1,)), dma((nx - 1,)),
-        dma((2, half, nx)), dma((2, half, nx)), dma((2, 8)), dma((2, 8)), dma((nx - 1,)), dma((nx - 1,)),
-        dma((8,)), dma((8,)), dma((2,)), dma((2,)),
+        vmem((nx, lines, 128), F32), vmem((3 * nx, nx, lines, 128), F32), vmem((2, 3 * nx, lines, 128), F32), vmem((8, 128), F32),
+        vmem((2, 1, 128), F32), vmem((nf, 1, 128), F32), vmem((ns, 1, 128), F32),
+        dma((6,)), dma, dma((nx - 1,)), dma, dma, dma, dma,
+        dma, dma((2, half, nx)), dma((3,)), dma((3,)), dma, dma, dma, dma((2,)), dma((2,)), dma((2,)),
     ]
     wide_out = jax.ShapeDtypeStruct(wide, F32)
     out = jax.ShapeDtypeStruct((cx, cy, cz), F32)
@@ -498,9 +533,9 @@
     operands = (x0, c, b, j, owner.reshape(lines, 128), slot.reshape(lines, 128))
     state = pl.pallas_call(
         functools.partial(body, nx, ny, nz),
-        out_shape=(wide_out,) * 5 + (out, jax.ShapeDtypeStruct((8, 128), F32)),
+        out_shape=(jax.ShapeDtypeStruct((2,) + wide, F32),) + (wide_out,) * 3 + (out, jax.ShapeDtypeStruct((8, 128), F32)),
         in_specs=[pl.BlockSpec(memory_space=pltpu.HBM)] * 6,
-        out_specs=(whole,) * 7,
+        out_specs=(whole,) * 6,
         scratch_shapes=scratch,
         compiler_params=pltpu.CompilerParams(collective_id=0, has_side_effects=True, vmem_limit_bytes=44 * 2**20),
         name="coupling_step",
@@ -510,7 +545,7 @@
         finish,
         grid=(cx // 8,),
         out_shape=(out, out),
-        in_specs=[whole] * 7,
+        in_specs=[whole] * 6,
         out_specs=(chunk, chunk),
         compiler_params=pltpu.CompilerParams(vmem_limit_bytes=16 * 2**20),
         name="finish_step",

time: 58.7 us -> 54.5 us (0.928)
  Pallas kernels: 57.9 us -> 53.7 us
    pallas_call x1, Pallas kernels: 56.3 us -> 52.1 us  [per_device(): pl.pallas_call(functools.partial(body, nx, ny, nz), out_shape=(jax.ShapeD...]
where the time goes in v3:
time: 54.5 us; the launch traced here: 54.4 us
  Pallas kernels  53.7 us (99%)
  between operations  0.64 us (1%)
    pallas_call x1, Pallas kernels, per_device(): pl.pallas_call(functools.partial(body, nx, ny, nz), out_shape=(jax.ShapeD...  52.1 us
    pallas_call x1, Pallas kernels, per_device(): pl.pallas_call(finish, grid=(cx // 8,), out_shape=(out, out), in_specs=[w...  1.59 us

profile of v3, /device:TPU:1, one launch (start us, length us, event | category | flops | bytes accessed | tf_op | source)
XLA Modules:
  0.0 54.4 jit_solution(7577056857431727756)
XLA Ops:
  0.6 52.1 %coupling_step.1 = (f32[2,42,48,128]{3,2,1,0:T(8,128)S(1)}, f32[42,48,128]{2,1,0:T(8,128)S(1)}, f32[42,48,128]{2,1,0:T(8,128)S(1)}, f32[42,48,128]{2,1,0:T(8,128...) custom-call(f32[32,32,128]{2,1,0:T(8,128)} %x0_hbm.1, f32[32,32,128]{2,1,0:T(8,128)} %c_hbm.1, f32[64,512]{1,0:T(8,128)} %b_hbm.1, ...), custom_call_target="tpu_custom_call" | custom-call | tf_op jit(solution)/shard_map/coupling_step/pallas_call | solution.py:534
  52.8 1.6 %finish_step.1 = (f32[32,32,128]{2,1,0:T(8,128)}, f32[32,32,128]{2,1,0:T(8,128)}) custom-call(f32[2,42,48,128]{3,2,1,0:T(8,128)S(1)} %get-tuple-element.8.field, f32[42,48,128]{2,1,0:T(8,128)S(1)} %get-tuple-element.9.w0, f32[42,48,128]{2,1,0:T(8,128)S(1)} %get-tuple-element.10.w1, f32[42,48,128]{2,1,0:T(8,128)S(1)} %get-tuple-element.11.w2, ...), custom_call_target="tpu_custom_call" | custom-call | tf_op jit(solution)/shard_map/finish_step/pallas_call | solution.py:544

commit v4 on v3

--- a/solution.py
+++ b/solution.py
@@ -29,7 +29,7 @@
     bv, jv, idx, tabs, held, jac, codes, code_own, key, jm, acc,
     part_out, part_in, cross_in, edge, sum_out, sum_plane, sum_line,
     load_sem, bx_send, bx_recv, jx_send, jx_recv, cx_send, cx_recv,
-    ring_send, ring_recv, halo_send, halo_recv, row_send, row_recv, cross_send, cross_recv, ar_send, ar_recv,
+    ring_send, ring_recv, halo_send, halo_recv, row_send, row_recv, cross_send, cross_recv, ar_send, ar_recv, tokens,
 ):
     xe, de = field.at[0], field.at[1]
     cx, cy, cz = (xe.shape[0] - 10, xe.shape[1] - 16, xe.shape[2])
@@ -80,28 +80,25 @@
         load.start()
 
     barrier = pltpu.get_barrier_semaphore()
-    partners = [on_x(d) for d in range(1, nx)] + [on_line(n) for n in range(1, ns)]
-    partners += [in_row(0, d, b) for d in range(1, nx) for b in (-1, 1)]
-    partners += [on_y(1), on_y(ny - 1)] + [beside(a, b) for a, b in AROUND if a != 0]
+    partners = [on_x(d) for d in range(1, nx)] + [on_y(1), on_y(ny - 1), beside(0, -1), beside(0, 1)]
     for at in partners:
         pl.semaphore_signal(barrier, inc=1, device_id=at, device_id_type=MESH)
 
-    @pl.when(x == 0)
-    def _():
-        for b in (-1, 0, 1):
-            for d in range(nx):
-                pl.semaphore_signal(barrier, inc=1, device_id=in_row(-1, d, b), device_id_type=MESH)
-
-    @pl.when(x == nx - 1)
-    def _():
-        for b in (-1, 0, 1):
-            for d in range(nx):
-                pl.semaphore_signal(barrier, inc=1, device_id=in_row(1, d, b), device_id_type=MESH)
+    def tell(kind, low, high):
+        pl.semaphore_signal(tokens.at[kind, 0], inc=1, device_id=low, device_id_type=MESH)
+        pl.semaphore_signal(tokens.at[kind, 1], inc=1, device_id=high, device_id_type=MESH)
+
+    def hear(kind):
+        pl.semaphore_wait(tokens.at[kind, 0], 1)
+        pl.semaphore_wait(tokens.at[kind, 1], 1)
 
     guard = jnp.zeros(xe.shape[1:], F32)
     for ref in (xe, w0, w1, w2):
         ref[0] = guard
         ref[cx + 9] = guard
+
+    for end in (0, nx * rowsets + 1):
+        part_out[end] = jnp.zeros((1, 128), F32)
 
     with jax.named_scope("tables"):
         loads[0].wait()
@@ -126,7 +123,8 @@
         loads[5].wait()
 
     with jax.named_scope("entry"):
-        pl.semaphore_wait(barrier, len(partners) + 6)
+        pl.semaphore_wait(barrier, len(partners))
+        tell(0, beside(0, -1), beside(0, 1))
 
     spread = []
     for d in range(1, nx):
@@ -222,7 +220,7 @@
             for k in range(tall // 128):
                 line = jnp.sum(product[k * 128 : (k + 1) * 128].T, axis=0, keepdims=True)
                 at = i * (tall // 128) + k
-                part_out[lax.rem(x - d + nx, nx), pl.ds(at, 1), :] = line
+                part_out[1 + lax.rem(x - d + nx, nx) * rowsets + at] = line
 
     def around_sum(ref, r, n):
         mid = ref[pl.ds(r, n)].reshape(n * xe.shape[1], cz)
@@ -264,59 +262,103 @@
         lax.fori_loop(0, (cx + 8) // 8, one, 0)
 
     order = sorted(range(nx), key=lambda d: (min(d, nx - d), -d))
-    for d in order:
-        if d == order[1]:
+
+    def round_of(t):
+        others = [(t, d) for d in order if d > 0]
+        ahead = [(t + 2, 0)] if t + 2 <= half else []
+        return ([(2, 0)] if t == 1 and half > 1 else []) + others + ahead
+
+    prepare_keys(0)
+    for n, (t, d) in enumerate(round_of(1)):
+        with jax.named_scope(f"forward#t={t}#d={d}"):
+            forward(t, d)
+        if (t, d) == (1, order[1]):
             coded.wait_recv()
-        if d > 0:
-            with jax.named_scope(f"forward#t=1#d={d}"):
-                forward(1, d)
-        with jax.named_scope(f"prepare_keys#d={d}"):
+        if t == 1:
             prepare_keys(d)
-
+    with jax.named_scope("hear#k=0"):
+        hear(0)
+    tell(1, on_y(ny - 1), on_y(1))
+    if ns > 4:
+        tell(2, beside(0, -2), beside(0, 2))
     for d in range(1, nx):
         to = lax.rem(x + d, nx)
         remote(
             jv.at[pl.ds(pl.multiple_of(to * share, share), share)], jac.at[d], jx_send, jx_recv, on_x(d)
         ).start()
-    to_x = {-1: (pl.ds(LOW, 4), pl.ds(LOW + cx, 4)), 0: (pl.ds(LOW, cx),) * 2, 1: (pl.ds(LOW + cx - 4, 4), pl.ds(LOW - 4, 4))}
     to_y = {-1: (pl.ds(SIDE, 8), pl.ds(SIDE + cy, 8)), 0: (pl.ds(SIDE, cy),) * 2, 1: (pl.ds(SIDE + cy - 8, 8), pl.ds(SIDE - 8, 8))}
-    def group(a, b):
-        return 0 if a == 0 else 1 if b == 0 else 2
-
-    def send_halos(groups):
-        for a, b in AROUND:
-            k = group(a, b)
-            if k in groups:
-                remote(
-                    field.at[:, to_x[a][0], to_y[b][0]], field.at[:, to_x[a][1], to_y[b][1]],
-                    halo_send.at[k], halo_recv.at[k], beside(a, b),
-                ).start()
-
+
+    def send_side(a):
+        def rows_of(count):
+            if a == 1:
+                return pl.ds(LOW + cx - count, count), pl.ds(LOW - count, count)
+            return pl.ds(LOW, count), pl.ds(LOW + cx, count)
+
+        near, near_to = rows_of(3)
+        four, four_to = rows_of(4)
+        fourth = pl.ds(LOW + cx - 4 if a == 1 else LOW + 3, 1)
+        fourth_to = pl.ds(LOW - 4 if a == 1 else LOW + cx + 3, 1)
+        sides = pl.ds(SIDE, cy)
+        cuts = [
+            (field.at[:, near, sides], field.at[:, near_to, sides], 1, 0),
+            (field.at[0, fourth, sides], field.at[0, fourth_to, sides], 2, 0),
+            (field.at[:, near, pl.ds(SIDE + cy - 4, 4)], field.at[:, near_to, pl.ds(SIDE - 4, 4)], 3, 1),
+            (field.at[:, near, pl.ds(SIDE, 4)], field.at[:, near_to, pl.ds(SIDE + cy, 4)], 3, -1),
+        ]
+        for src, dst, k, b in cuts:
+            remote(src, dst, halo_send.at[k], halo_recv.at[k], beside(a, b)).start()
+
+    ends = ((1, nx - 1), (-1, 0))
+
+    def send_sides(inside):
+        for a, end in ends:
+            @pl.when((x != end) if inside else (x == end))
+            def _():
+                send_side(a)
+
+    for b in (-1, 1):
+        remote(
+            field.at[:, pl.ds(LOW, cx), to_y[b][0]], field.at[:, pl.ds(LOW, cx), to_y[b][1]],
+            halo_send.at[0], halo_recv.at[0], beside(0, b),
+        ).start()
+    send_sides(True)
     rims = [
         field.at[:, pl.ds(LOW, cx), pl.ds(0, 16)],
-        field.at[:, pl.ds(LOW - 4, 8), pl.ds(SIDE, cy)],
-        field.at[:, pl.ds(LOW - 4, 8), pl.ds(0, 16)],
+        field.at[:, pl.ds(LOW - 3, 6), pl.ds(SIDE, cy)],
+        field.at[0, pl.ds(LOW - 4, 2), pl.ds(SIDE, cy)],
+        field.at[:, pl.ds(LOW - 3, 6), pl.ds(0, 8)],
     ]
     halos = [remote(rim, rim, halo_send.at[k], halo_recv.at[k], on_x(1)) for k, rim in enumerate(rims)]
-    send_halos((0,))
 
     def near(far):
         if far == 0:
             return [y]
         return [lax.rem(y + ny - far, ny), lax.rem(y + far, ny)]
 
+    def hear_more():
+        hear(1)
+        if ns > 4:
+            hear(2)
+        if ns > 8:
+            tell(3, beside(0, -4), beside(0, 4))
+
     for t in range(2, half + 1):
-        for d in order:
-            with jax.named_scope(f"forward#t={t}#d={d}"):
-                forward(t, d)
+        todo = round_of(t)
+        for n, d in enumerate(order):
+            if n < len(todo):
+                with jax.named_scope(f"forward#t={t}#n={n}"):
+                    forward(*todo[n])
             with jax.named_scope(f"pick#t={t}#d={d}"):
                 pick(d, near(t - 2), first=t == 2)
-            if t == half:
+            if t == max(2, half - 1):
                 if d == 0:
+                    hear_more()
                     jacs.wait_recv()
                 with jax.named_scope(f"prepare_jac#d={d}"):
                     prepare_jac(d)
-    send_halos((1, 2))
+    send_sides(False)
+    if half == 1:
+        hear_more()
     if half == 1:
         jacs.wait_recv()
         for d in range(nx):
@@ -324,6 +366,9 @@
     for d in range(nx):
         with jax.named_scope(f"pick_near#d={d}"):
             pick(d, near(half - 1), first=half == 1)
+    if ns > 8:
+        with jax.named_scope("hear#k=3"):
+            hear(3)
     with jax.named_scope("far_wait"):
         for d in range(nx):
             for way in range(2):
@@ -333,14 +378,17 @@
         with jax.named_scope(f"pick_far#d={d}"):
             pick(d, [lax.rem(y + half, ny)], finish=True)
 
-    part_in[nx + x] = part_out[...]
+    part_in[nx + x] = part_out[pl.ds(x * rowsets, rowsets + 2)]
     for b in (-1, 0, 1):
         slot = (1 - b) * nx + x
-        remote(part_out.at[nx - 1], cross_in.at[0, slot], cross_send, cross_recv.at[0], in_row(1, nx - x, b)).start()
-        remote(part_out.at[0], cross_in.at[1, slot], cross_send, cross_recv.at[1], in_row(-1, 2 * nx - 1 - x, b)).start()
         for d in range(nx):
             if (d, b) != (0, 0):
-                remote(part_out, part_in.at[slot], row_send, row_recv, in_row(0, d, b)).start()
+                lines = part_out.at[pl.ds(lax.rem(x + d, nx) * rowsets, rowsets + 2)]
+                remote(lines, part_in.at[slot], row_send, row_recv, in_row(0, d, b)).start()
+        line = part_out.at[nx * rowsets]
+        remote(line, cross_in.at[0, slot], cross_send, cross_recv.at[0], in_row(1, nx - x, b)).start()
+        line = part_out.at[1]
+        remote(line, cross_in.at[1, slot], cross_send, cross_recv.at[1], in_row(-1, 2 * nx - 1 - x, b)).start()
     most = part_in.at[pl.ds(0, 3 * nx - 1)]
     rows_all = remote(most, most, row_send, row_recv, on_x(1))
     six = cross_in.at[0, pl.ds(0, 6)]
@@ -370,21 +418,21 @@
         here = (pl.ds(r, per), pl.ds(first, count))
         w0[here] = w0[here] + jnp.where(spot == cz - 1, column * de[here], 0.0)
 
-    def gathered(b, reader, spots):
-        return sum(part_in[(b + 1) * nx + h, reader, spots, :] for h in range(nx))
+    def gathered(b, spot):
+        return sum(part_in[(b + 1) * nx + h, spot] for h in range(nx))
 
     with jax.named_scope("heat"):
-        for a, end, side, spot in ((1, nx - 1, 1, 0), (-1, 0, 0, cx // per - 1)):
+        for a, end, side, spot in ((1, nx - 1, 1, rowsets + 1), (-1, 0, 0, 0)):
             for b in (-1, 0, 1):
                 here = pl.ds(3 * side + b + 1, 1)
 
                 @pl.when(x == end)
                 def _():
-                    edge[here, :] = sum(cross_in[side, (b + 1) * nx + h, spot : spot + 1, :] for h in range(nx))
+                    edge[here, :] = sum(cross_in[side, (b + 1) * nx + h] for h in range(nx))
 
                 @pl.when(x != end)
                 def _():
-                    edge[here, :] = gathered(b, lax.rem(x + a + nx, nx), slice(spot, spot + 1))
+                    edge[here, :] = gathered(b, spot)
 
         for a in (-1, 0, 1):
             for b in (-1, 0, 1):
@@ -392,9 +440,8 @@
                 count = {0: cy, -1: 8, 1: 8}[b]
                 offset = {0: 0, -1: cy - 8, 1: 0}[b]
                 if a == 0:
-                    block = gathered(b, x, slice(0, cx // per))
                     for i in range(cx // per):
-                        heat(LOW + i * per, first, count, block[i : i + 1], offset)
+                        heat(LOW + i * per, first, count, gathered(b, 1 + i), offset)
                 else:
                     at = 3 * (1 if a == 1 else 0) + b + 1
                     heat(LOW + cx if a == 1 else LOW - 4, first, count, edge[at : at + 1, :], offset)
@@ -522,10 +569,11 @@
         vmem((nx, deep, 128), F32), vmem((ny, nx, deep, 128), F32), vmem((nx, share, rows), F32),
         vmem((nx, lines, 128), jnp.int32), vmem((lines, 128), jnp.int32),
         vmem((nx * rows, 128), F32), vmem((nx * rows, 128), F32), vmem((nx * rows, 128), F32),
-        vmem((nx, lines, 128), F32), vmem((3 * nx, nx, lines, 128), F32), vmem((2, 3 * nx, lines, 128), F32), vmem((8, 128), F32),
+        vmem((nx * lines + 2, 1, 128), F32), vmem((3 * nx, lines + 2, 1, 128), F32), vmem((2, 3 * nx, 1, 128), F32), vmem((8, 128), F32),
         vmem((2, 1, 128), F32), vmem((nf, 1, 128), F32), vmem((ns, 1, 128), F32),
         dma((6,)), dma, dma((nx - 1,)), dma, dma, dma, dma,
-        dma, dma((2, half, nx)), dma((3,)), dma((3,)), dma, dma, dma, dma((2,)), dma((2,)), dma((2,)),
+        dma, dma((2, half, nx)), dma((4,)), dma((4,)), dma, dma, dma, dma((2,)), dma((2,)), dma((2,)),
+        pltpu.SemaphoreType.REGULAR((4, 2)),
     ]
     wide_out = jax.ShapeDtypeStruct(wide, F32)
     out = jax.ShapeDtypeStruct((cx, cy, cz), F32)

time: 54.5 us -> 53 us (0.972)
  Pallas kernels: 53.7 us -> 52.2 us
    pallas_call x1, Pallas kernels: 52.1 us -> 50.6 us  [per_device(): pl.pallas_call(functools.partial(body, nx, ny, nz), out_shape=(jax.ShapeD...]
where the time goes in v4:
time: 53 us; the launch traced here: 52.8 us
  Pallas kernels  52.2 us (98%)
  between operations  0.64 us (1%)
    pallas_call x1, Pallas kernels, per_device(): pl.pallas_call(functools.partial(body, nx, ny, nz), out_shape=(jax.ShapeD...  50.6 us
    pallas_call x1, Pallas kernels, per_device(): pl.pallas_call(finish, grid=(cx // 8,), out_shape=(out, out), in_specs=[w...  1.59 us

profile of v4, /device:TPU:1, one launch (start us, length us, event | category | flops | bytes accessed | tf_op | source)
XLA Modules:
  0.0 52.8 jit_solution(5709560970715746485)
XLA Ops:
  0.6 50.6 %coupling_step.1 = (f32[2,42,48,128]{3,2,1,0:T(8,128)S(1)}, f32[42,48,128]{2,1,0:T(8,128)S(1)}, f32[42,48,128]{2,1,0:T(8,128)S(1)}, f32[42,48,128]{2,1,0:T(8,128...) custom-call(f32[32,32,128]{2,1,0:T(8,128)} %x0_hbm.1, f32[32,32,128]{2,1,0:T(8,128)} %c_hbm.1, f32[64,512]{1,0:T(8,128)} %b_hbm.1, ...), custom_call_target="tpu_custom_call" | custom-call | tf_op jit(solution)/shard_map/coupling_step/pallas_call | solution.py:582
  51.2 1.6 %finish_step.1 = (f32[32,32,128]{2,1,0:T(8,128)}, f32[32,32,128]{2,1,0:T(8,128)}) custom-call(f32[2,42,48,128]{3,2,1,0:T(8,128)S(1)} %get-tuple-element.8.field, f32[42,48,128]{2,1,0:T(8,128)S(1)} %get-tuple-element.9.w0, f32[42,48,128]{2,1,0:T(8,128)S(1)} %get-tuple-element.10.w1, f32[42,48,128]{2,1,0:T(8,128)S(1)} %get-tuple-element.11.w2, ...), custom_call_target="tpu_custom_call" | custom-call | tf_op jit(solution)/shard_map/finish_step/pallas_call | solution.py:592

commit v5 on v4

--- a/solution.py
+++ b/solution.py
@@ -61,8 +61,8 @@
     def in_row(a, d, b):
         return (lax.rem(y + a + ny, ny) * nx + lax.rem(x + d, nx), lax.rem(s + b + ns, ns))
 
-    def on_plane(n):
-        return (lax.rem(f + n, nf), s)
+    def on_plane(d, e):
+        return (lax.rem(y + e, ny) * nx + lax.rem(x + d, nx), s)
 
     def on_line(n):
         return (f, lax.rem(s + n, ns))
@@ -117,15 +117,37 @@
         code_own[...] = idx[0] * faces + idx[1]
         codes[0] = code_own[...]
         held[y, 0] = tabs[x]
-        loads[3].wait()
-        jac[0] = jv[pl.ds(pl.multiple_of(x * share, share), share), :]
-        loads[4].wait()
-        loads[5].wait()
 
     with jax.named_scope("entry"):
         pl.semaphore_wait(barrier, len(partners))
         tell(0, beside(0, -1), beside(0, 1))
 
+    def ring(t, d, way):
+        slot = lax.rem(y + ny + (1 - t if way == 0 else t - 1), ny)
+        at = on_y(1 if way == 0 else ny - 1)
+        block = held.at[slot, d]
+        return remote(block, block, ring_send, ring_recv.at[way, t - 1, d], at)
+
+    half = ny // 2
+
+    def goes(t, d, way):
+        return t < half or (d < nx // 2) == (way == 0)
+
+    ways = [
+        [[ring(t, d, way) if goes(t, d, way) else None for way in range(2)] for d in range(nx)]
+        for t in range(1, half + 1)
+    ]
+
+    def forward(t, d):
+        if t == 1 and d > 0:
+            spread[d - 1].wait_recv()
+        for way in range(2):
+            if t > 1:
+                ways[t - 2][d][way].wait_recv()
+            if goes(t, d, way):
+                ways[t - 1][d][way].start()
+
+    forward(1, 0)
     spread = []
     for d in range(1, nx):
         remote(code_own, codes.at[d], cx_send, cx_recv, on_x(d)).start()
@@ -139,32 +161,6 @@
         spread.append(remote(tabs.at[to], held.at[y, d], bx_send, bx_recv.at[d - 1], on_x(d)))
         spread[-1].start()
 
-    def ring(t, d, way):
-        slot = lax.rem(y + ny + (1 - t if way == 0 else t - 1), ny)
-        at = on_y(1 if way == 0 else ny - 1)
-        block = held.at[slot, d]
-        return remote(block, block, ring_send, ring_recv.at[way, t - 1, d], at)
-
-    half = ny // 2
-
-    def goes(t, d, way):
-        return t < half or (d < nx // 2) == (way == 0)
-
-    ways = [
-        [[ring(t, d, way) if goes(t, d, way) else None for way in range(2)] for d in range(nx)]
-        for t in range(1, half + 1)
-    ]
-
-    def forward(t, d):
-        if t == 1 and d > 0:
-            spread[d - 1].wait_recv()
-        for way in range(2):
-            if t > 1:
-                ways[t - 2][d][way].wait_recv()
-            if goes(t, d, way):
-                ways[t - 1][d][way].start()
-
-    forward(1, 0)
     def prepare_keys(d):
         for i in range(rowsets):
             code = codes[d, i : i + 1, :]
@@ -194,7 +190,7 @@
 
     tall = 512
 
-    def pick(d, slots, first=False, finish=False):
+    def pick(d, slots, first=False, finish=None):
         table = jnp.concatenate([weight(slot) for slot in slots], axis=0)
         lanes = iota((1, 128), 1)
         marks = []
@@ -206,21 +202,22 @@
                     mark = jnp.where(lanes // deep == e, base_of(slot, p) + lanes - e * deep, mark)
                 marks.append(mark.astype(F32))
         for i in range(rows // tall):
-            place = pl.ds(d * rows + i * tall, tall)
+            start = d * rows + i * tall
+            place = pl.ds(start if isinstance(start, int) else pl.multiple_of(start, tall), tall)
             keys = key[place, :]
             hot = jnp.concatenate([jnp.where(keys == mark, 1.0, 0.0).astype(BF16) for mark in marks], axis=1)
             both = jnp.dot(hot, table, preferred_element_type=F32)
             got = both[:, :128] + both[:, 128:]
             if not first:
                 got = got + acc[place, :]
-            if not finish:
+            if finish is None:
                 acc[place, :] = got
                 continue
             product = got * jm[place, :]
             for k in range(tall // 128):
                 line = jnp.sum(product[k * 128 : (k + 1) * 128].T, axis=0, keepdims=True)
                 at = i * (tall // 128) + k
-                part_out[1 + lax.rem(x - d + nx, nx) * rowsets + at] = line
+                part_out[1 + finish * rowsets + at] = line
 
     def around_sum(ref, r, n):
         mid = ref[pl.ds(r, n)].reshape(n * xe.shape[1], cz)
@@ -278,6 +275,9 @@
             prepare_keys(d)
     with jax.named_scope("hear#k=0"):
         hear(0)
+        for load in loads[3:]:
+            load.wait()
+        jac[0] = jv[pl.ds(pl.multiple_of(x * share, share), share), :]
     tell(1, on_y(ny - 1), on_y(1))
     if ns > 4:
         tell(2, beside(0, -2), beside(0, 2))
@@ -335,6 +335,14 @@
             return [y]
         return [lax.rem(y + ny - far, ny), lax.rem(y + far, ny)]
 
+    unprepared = list(order)
+
+    def next_jac():
+        with jax.named_scope(f"prepare_jac#n={len(unprepared)}"):
+            if len(unprepared) == nx:
+                jacs.wait_recv()
+            prepare_jac(unprepared.pop(0))
+
     def hear_more():
         hear(1)
         if ns > 4:
@@ -350,19 +358,15 @@
                     forward(*todo[n])
             with jax.named_scope(f"pick#t={t}#d={d}"):
                 pick(d, near(t - 2), first=t == 2)
-            if t == max(2, half - 1):
-                if d == 0:
-                    hear_more()
-                    jacs.wait_recv()
-                with jax.named_scope(f"prepare_jac#d={d}"):
-                    prepare_jac(d)
+            if t == max(2, half - 1) and n == 0:
+                hear_more()
+            if (t == half - 1 and n % 2 == 1) or (t == half and n < 2):
+                next_jac()
     send_sides(False)
     if half == 1:
         hear_more()
-    if half == 1:
-        jacs.wait_recv()
-        for d in range(nx):
-            prepare_jac(d)
+    while unprepared:
+        next_jac()
     for d in range(nx):
         with jax.named_scope(f"pick_near#d={d}"):
             pick(d, near(half - 1), first=half == 1)
@@ -374,21 +378,30 @@
             for way in range(2):
                 if goes(half, d, way):
                     ways[half - 1][d][way].wait_recv()
-    for d in range(nx):
-        with jax.named_scope(f"pick_far#d={d}"):
-            pick(d, [lax.rem(y + half, ny)], finish=True)
-
-    part_in[nx + x] = part_out[pl.ds(x * rowsets, rowsets + 2)]
-    for b in (-1, 0, 1):
+    def share_ends(b):
         slot = (1 - b) * nx + x
-        for d in range(nx):
-            if (d, b) != (0, 0):
-                lines = part_out.at[pl.ds(lax.rem(x + d, nx) * rowsets, rowsets + 2)]
-                remote(lines, part_in.at[slot], row_send, row_recv, in_row(0, d, b)).start()
         line = part_out.at[nx * rowsets]
         remote(line, cross_in.at[0, slot], cross_send, cross_recv.at[0], in_row(1, nx - x, b)).start()
         line = part_out.at[1]
         remote(line, cross_in.at[1, slot], cross_send, cross_recv.at[1], in_row(-1, 2 * nx - 1 - x, b)).start()
+
+    def share_rows(b):
+        slot = (1 - b) * nx + x
+        for d in order[::-1]:
+            if (d, b) != (0, 0):
+                lines = part_out.at[pl.ds(lax.rem(x + d, nx) * rowsets, rowsets + 2)]
+                remote(lines, part_in.at[slot], row_send, row_recv, in_row(0, d, b)).start()
+
+    readers = [0, nx - 1] + list(range(1, nx - 1))
+    for n, reader in enumerate(readers):
+        with jax.named_scope(f"pick_far#d={reader}"):
+            pick(lax.rem(x - reader + nx, nx), [lax.rem(y + half, ny)], finish=reader)
+        if n == 2:
+            for b in (1, -1, 0):
+                share_ends(b)
+    for b in (1, -1, 0):
+        share_rows(b)
+    part_in[nx + x] = part_out[pl.ds(x * rowsets, rowsets + 2)]
     most = part_in.at[pl.ds(0, 3 * nx - 1)]
     rows_all = remote(most, most, row_send, row_recv, on_x(1))
     six = cross_in.at[0, pl.ds(0, 6)]
@@ -468,7 +481,7 @@
             return (odd, even)
 
         zero = jnp.zeros((8, cz), F32)
-        sums = lax.fori_loop(0, cx // 8, one, (zero,) * (3 if first else 2))
+        sums = lax.fori_loop(0, cx // 8, one, (zero,) * (3 if first else 2), unroll=True)
         for r in (LOW - 4, LOW + cx):
             new[pl.ds(r, 4)] = de[pl.ds(r, 4)] * around_sum(ref, r, 4)
         return sums
@@ -484,7 +497,7 @@
         return carry + fold(inside(w2[pl.ds(LOW + 8 * i, 8)]) * near)
 
     with jax.named_scope("step#k=2"):
-        mu5 = lax.fori_loop(0, cx // 8, final, jnp.zeros((8, cz), F32))
+        mu5 = lax.fori_loop(0, cx // 8, final, jnp.zeros((8, cz), F32), unroll=True)
     lines = [jnp.sum(v, axis=0, keepdims=True) for v in (mu0, mu1, mu2, mu3, mu4, mu5)]
     lines.append(jnp.zeros((2, cz), F32))
     sums = jnp.sum(jnp.concatenate(lines, axis=0), axis=1, keepdims=True)
@@ -502,10 +515,13 @@
         sends.append(everyone)
         return jnp.sum(slots[...], axis=0)
 
+    others = [(d, e) for d in range(nx) for e in range(ny) if (d, e) != (0, 0)]
+    others.sort(key=lambda o: -min(o[0], nx - o[0]) - min(o[1], ny - o[1]))
+    far_first = sorted(range(1, ns), key=lambda n: -min(n, ns - n))
     with jax.named_scope("reduce#k=0"):
-        local = reduce(0, local, sum_plane, f, [on_plane(n) for n in range(1, nf)])
+        local = reduce(0, local, sum_plane, f, [on_plane(d, e) for d, e in others])
     with jax.named_scope("reduce#k=1"):
-        local = reduce(1, local, sum_line, s, [on_line(n) for n in range(1, ns)])
+        local = reduce(1, local, sum_line, s, [on_line(n) for n in far_first])
     lane = iota((1, 128), 1)
     mu = [jnp.sum(jnp.where(lane == k, local, 0.0), axis=1, keepdims=True) for k in range(6)]
     mu = [jnp.broadcast_to(m, (1, 128)) for m in mu]

time: 53 us -> 51.9 us (0.979)
  Pallas kernels: 52.2 us -> 51.1 us
    pallas_call x1, Pallas kernels: 50.6 us -> 49.5 us  [per_device(): pl.pallas_call(functools.partial(body, nx, ny, nz), out_shape=(jax.ShapeD...]
where the time goes in v5:
time: 51.9 us; the launch traced here: 51.7 us
  Pallas kernels  51.1 us (98%)
  between operations  0.64 us (1%)
    pallas_call x1, Pallas kernels, per_device(): pl.pallas_call(functools.partial(body, nx, ny, nz), out_shape=(jax.ShapeD...  49.5 us
    pallas_call x1, Pallas kernels, per_device(): pl.pallas_call(finish, grid=(cx // 8,), out_shape=(out, out), in_specs=[w...  1.59 us

profile of v5, /device:TPU:1, one launch (start us, length us, event | category | flops | bytes accessed | tf_op | source)
XLA Modules:
  0.0 51.7 jit_solution(8466599773709643547)
XLA Ops:
  0.6 49.5 %coupling_step.1 = (f32[2,42,48,128]{3,2,1,0:T(8,128)S(1)}, f32[42,48,128]{2,1,0:T(8,128)S(1)}, f32[42,48,128]{2,1,0:T(8,128)S(1)}, f32[42,48,128]{2,1,0:T(8,128...) custom-call(f32[32,32,128]{2,1,0:T(8,128)} %x0_hbm.1, f32[32,32,128]{2,1,0:T(8,128)} %c_hbm.1, f32[64,512]{1,0:T(8,128)} %b_hbm.1, ...), custom_call_target="tpu_custom_call" | custom-call | tf_op jit(solution)/shard_map/coupling_step/pallas_call | solution.py:598
  50.1 1.6 %finish_step.1 = (f32[32,32,128]{2,1,0:T(8,128)}, f32[32,32,128]{2,1,0:T(8,128)}) custom-call(f32[2,42,48,128]{3,2,1,0:T(8,128)S(1)} %get-tuple-element.8.field, f32[42,48,128]{2,1,0:T(8,128)S(1)} %get-tuple-element.9.w0, f32[42,48,128]{2,1,0:T(8,128)S(1)} %get-tuple-element.10.w1, f32[42,48,128]{2,1,0:T(8,128)S(1)} %get-tuple-element.11.w2, ...), custom_call_target="tpu_custom_call" | custom-call | tf_op jit(solution)/shard_map/finish_step/pallas_call | solution.py:608

commit v6 on v5

--- a/solution.py
+++ b/solution.py
@@ -29,7 +29,7 @@
     bv, jv, idx, tabs, held, jac, codes, code_own, key, jm, acc,
     part_out, part_in, cross_in, edge, sum_out, sum_plane, sum_line,
     load_sem, bx_send, bx_recv, jx_send, jx_recv, cx_send, cx_recv,
-    ring_send, ring_recv, halo_send, halo_recv, row_send, row_recv, cross_send, cross_recv, ar_send, ar_recv, tokens,
+    ring_send, ring_recv, halo_send, halo_recv, row_send, row_recv, cross_send, cross_recv, ar_send, ar_recv, tokens, tables,
 ):
     xe, de = field.at[0], field.at[1]
     cx, cy, cz = (xe.shape[0] - 10, xe.shape[1] - 16, xe.shape[2])
@@ -190,8 +190,11 @@
 
     tall = 512
 
-    def pick(d, slots, first=False, finish=None):
-        table = jnp.concatenate([weight(slot) for slot in slots], axis=0)
+    def pick(d, slots, fresh, first=False, finish=None):
+        if fresh:
+            for n, slot in enumerate(slots):
+                tables[n * nx * deep : (n + 1) * nx * deep, :] = weight(slot)
+        table = tables[: len(slots) * nx * deep, :]
         lanes = iota((1, 128), 1)
         marks = []
         for slot in slots:
@@ -357,7 +360,7 @@
                 with jax.named_scope(f"forward#t={t}#n={n}"):
                     forward(*todo[n])
             with jax.named_scope(f"pick#t={t}#d={d}"):
-                pick(d, near(t - 2), first=t == 2)
+                pick(d, near(t - 2), n == 0, first=t == 2)
             if t == max(2, half - 1) and n == 0:
                 hear_more()
             if (t == half - 1 and n % 2 == 1) or (t == half and n < 2):
@@ -369,7 +372,7 @@
         next_jac()
     for d in range(nx):
         with jax.named_scope(f"pick_near#d={d}"):
-            pick(d, near(half - 1), first=half == 1)
+            pick(d, near(half - 1), d == 0, first=half == 1)
     if ns > 8:
         with jax.named_scope("hear#k=3"):
             hear(3)
@@ -395,7 +398,7 @@
     readers = [0, nx - 1] + list(range(1, nx - 1))
     for n, reader in enumerate(readers):
         with jax.named_scope(f"pick_far#d={reader}"):
-            pick(lax.rem(x - reader + nx, nx), [lax.rem(y + half, ny)], finish=reader)
+            pick(lax.rem(x - reader + nx, nx), [lax.rem(y + half, ny)], n == 0, finish=reader)
         if n == 2:
             for b in (1, -1, 0):
                 share_ends(b)
@@ -589,7 +592,7 @@
         vmem((2, 1, 128), F32), vmem((nf, 1, 128), F32), vmem((ns, 1, 128), F32),
         dma((6,)), dma, dma((nx - 1,)), dma, dma, dma, dma,
         dma, dma((2, half, nx)), dma((4,)), dma((4,)), dma, dma, dma, dma((2,)), dma((2,)), dma((2,)),
-        pltpu.SemaphoreType.REGULAR((4, 2)),
+        pltpu.SemaphoreType.REGULAR((4, 2)), vmem((2 * nx * deep, 256), BF16),
     ]
     wide_out = jax.ShapeDtypeStruct(wide, F32)
     out = jax.ShapeDtypeStruct((cx, cy, cz), F32)
@@ -604,10 +607,10 @@
         compiler_params=pltpu.CompilerParams(collective_id=0, has_side_effects=True, vmem_limit_bytes=44 * 2**20),
         name="coupling_step",
     )(*[pltpu.with_memory_space_constraint(v, pltpu.HBM) for v in operands])
-    chunk = pl.BlockSpec((8, cy, cz), lambda i: (i, 0, 0))
+    chunk = pl.BlockSpec((cx // 2, cy, cz), lambda i: (i, 0, 0))
     return pl.pallas_call(
         finish,
-        grid=(cx // 8,),
+        grid=(2,),
         out_shape=(out, out),
         in_specs=[whole] * 6,
         out_specs=(chunk, chunk),

time: 51.9 us -> 51.3 us (0.988)
  Pallas kernels: 51.1 us -> 50.5 us
    pallas_call x1, Pallas kernels: 1.59 us -> 1.06 us  [per_device(): pl.pallas_call(finish, grid=(2,), out_shape=(out, out), in_specs=[whole]...]
where the time goes in v6:
time: 51.3 us; the launch traced here: 51.2 us
  Pallas kernels  50.5 us (98%)
  between operations  0.64 us (1%)
    pallas_call x1, Pallas kernels, per_device(): pl.pallas_call(functools.partial(body, nx, ny, nz), out_shape=(jax.ShapeD...  49.5 us
    pallas_call x1, Pallas kernels, per_device(): pl.pallas_call(finish, grid=(2,), out_shape=(out, out), in_specs=[whole]...  1.06 us

profile of v6, /device:TPU:1, one launch (start us, length us, event | category | flops | bytes accessed | tf_op | source)
XLA Modules:
  0.0 51.2 jit_solution(13134309713433949212)
XLA Ops:
  0.6 49.5 %coupling_step.1 = (f32[2,42,48,128]{3,2,1,0:T(8,128)S(1)}, f32[42,48,128]{2,1,0:T(8,128)S(1)}, f32[42,48,128]{2,1,0:T(8,128)S(1)}, f32[42,48,128]{2,1,0:T(8,128...) custom-call(f32[32,32,128]{2,1,0:T(8,128)} %x0_hbm.1, f32[32,32,128]{2,1,0:T(8,128)} %c_hbm.1, f32[64,512]{1,0:T(8,128)} %b_hbm.1, ...), custom_call_target="tpu_custom_call" | custom-call | tf_op jit(solution)/shard_map/coupling_step/pallas_call | solution.py:601
  50.1 1.1 %finish_step.1 = (f32[32,32,128]{2,1,0:T(8,128)}, f32[32,32,128]{2,1,0:T(8,128)}) custom-call(f32[2,42,48,128]{3,2,1,0:T(8,128)S(1)} %get-tuple-element.8.field, f32[42,48,128]{2,1,0:T(8,128)S(1)} %get-tuple-element.9.w0, f32[42,48,128]{2,1,0:T(8,128)S(1)} %get-tuple-element.10.w1, f32[42,48,128]{2,1,0:T(8,128)S(1)} %get-tuple-element.11.w2, ...), custom_call_target="tpu_custom_call" | custom-call | tf_op jit(solution)/shard_map/finish_step/pallas_call | solution.py:611

commit v7 on v6

--- a/solution.py
+++ b/solution.py
@@ -188,7 +188,7 @@
     def base_of(slot, d):
         return (slot * nx + lax.rem(x - d + nx, nx)) * deep
 
-    tall = 512
+    tall = rows
 
     def pick(d, slots, fresh, first=False, finish=None):
         if fresh:

time: 51.3 us -> 51.8 us (level)
  no operation moved by 1% of the time
where the time goes in v7:
time: 51.8 us; the launch traced here: 51.6 us
  Pallas kernels  51 us (98%)
  between operations  0.64 us (1%)
    pallas_call x1, Pallas kernels, per_device(): pl.pallas_call(functools.partial(body, nx, ny, nz), out_shape=(jax.ShapeD...  49.9 us
    pallas_call x1, Pallas kernels, per_device(): pl.pallas_call(finish, grid=(2,), out_shape=(out, out), in_specs=[whole]...  1.06 us

profile of v7, /device:TPU:1, one launch (start us, length us, event | category | flops | bytes accessed | tf_op | source)
XLA Modules:
  0.0 51.6 jit_solution(10796828635530241285)
XLA Ops:
  0.6 49.9 %coupling_step.1 = (f32[2,42,48,128]{3,2,1,0:T(8,128)S(1)}, f32[42,48,128]{2,1,0:T(8,128)S(1)}, f32[42,48,128]{2,1,0:T(8,128)S(1)}, f32[42,48,128]{2,1,0:T(8,128...) custom-call(f32[32,32,128]{2,1,0:T(8,128)} %x0_hbm.1, f32[32,32,128]{2,1,0:T(8,128)} %c_hbm.1, f32[64,512]{1,0:T(8,128)} %b_hbm.1, ...), custom_call_target="tpu_custom_call" | custom-call | tf_op jit(solution)/shard_map/coupling_step/pallas_call | solution.py:601
  50.6 1.1 %finish_step.1 = (f32[32,32,128]{2,1,0:T(8,128)}, f32[32,32,128]{2,1,0:T(8,128)}) custom-call(f32[2,42,48,128]{3,2,1,0:T(8,128)S(1)} %get-tuple-element.8.field, f32[42,48,128]{2,1,0:T(8,128)S(1)} %get-tuple-element.9.w0, f32[42,48,128]{2,1,0:T(8,128)S(1)} %get-tuple-element.10.w1, f32[42,48,128]{2,1,0:T(8,128)S(1)} %get-tuple-element.11.w2, ...), custom_call_target="tpu_custom_call" | custom-call | tf_op jit(solution)/shard_map/finish_step/pallas_call | solution.py:611
